TPU v7x, 8 devices: a whole 2x2x1 slice. The times are simulated.
8 devices in a mesh: row: 2 (over z, y), col: 4 (over x, core).
Axes of the slice: x: 2, y: 2, z: 1, core: 2. Of those that a mesh axis runs over, the one named last changes fastest.
Arguments:
- w_one: float32 [2, 4, 4, 384, 1536], P('row', 'col')
- w_two: float32 [2, 4, 4, 1536, 384], P('row', 'col')
- inputs: bfloat16 [2, 4, 3, 2048, 384], P('row', 'col')
- targets: bfloat16 [2, 4, 3, 2048, 384], P('row', 'col')
Outputs:
- output 1: float32 [2, 4, 4, 384, 1536], P('row', 'col')
- output 2: float32 [2, 4, 4, 1536, 384], P('row', 'col')
All inputs are finite; a program needn't handle non-finite values.
Results may differ from a plain program's by a relative error of at most 0.00188.
Values are sent between devices in bfloat16 or wider.
A program may use at most 1 GiB of HBM per device.

v0:
```python
import jax
import jax.numpy as jnp
from jax import lax
from jax.sharding import PartitionSpec as P

LEARN_RATE = 1.5
NORM_EPS = 1e-6
GELU_C = 0.7978845608028654
GELU_K = 0.044715


def gelu_value(pre_act):
    tanh_inner = jnp.tanh(GELU_C * (pre_act + GELU_K * pre_act * pre_act * pre_act))
    return 0.5 * pre_act * (1.0 + tanh_inner)


def gelu_slope(pre_act):
    tanh_inner = jnp.tanh(GELU_C * (pre_act + GELU_K * pre_act * pre_act * pre_act))
    return 0.5 * (1.0 + tanh_inner) + 0.5 * pre_act * (1.0 - tanh_inner * tanh_inner) * GELU_C * (1.0 + 3.0 * GELU_K * pre_act * pre_act)


def local_grads(one_list, two_list, x_in, target):
    n_layers = len(one_list)
    one_lo = [w.astype(jnp.bfloat16) for w in one_list]
    two_lo = [w.astype(jnp.bfloat16) for w in two_list]
    hidden = x_in
    saved_acts = []
    for layer_idx in range(n_layers):
        hid_f = hidden.astype(jnp.float32)
        inv_rms = lax.rsqrt(jnp.mean(hid_f * hid_f, axis=-1, keepdims=True) + NORM_EPS)
        normed = hid_f * inv_rms
        normed_lo = normed.astype(jnp.bfloat16)
        pre_act = jnp.dot(normed_lo, one_lo[layer_idx], preferred_element_type=jnp.float32)
        act_lo = gelu_value(pre_act).astype(jnp.bfloat16)
        mlp_out = jnp.dot(act_lo, two_lo[layer_idx], preferred_element_type=jnp.float32)
        saved_acts.append((normed, inv_rms, normed_lo, pre_act, act_lo))
        hidden = (hid_f + mlp_out).astype(jnp.bfloat16)
    loss_scale = 2.0 / (x_in.shape[0] * x_in.shape[1])
    d_hidden = loss_scale * (hidden.astype(jnp.float32) - target.astype(jnp.float32))
    grads_one = [None] * n_layers
    grads_two = [None] * n_layers
    for layer_idx in reversed(range(n_layers)):
        normed, inv_rms, normed_lo, pre_act, act_lo = saved_acts[layer_idx]
        d_lo = d_hidden.astype(jnp.bfloat16)
        grads_two[layer_idx] = jnp.einsum('bf,bd->fd', act_lo, d_lo, preferred_element_type=jnp.float32)
        d_act = jnp.einsum('bd,fd->bf', d_lo, two_lo[layer_idx], preferred_element_type=jnp.float32)
        d_pre = (d_act * gelu_slope(pre_act)).astype(jnp.bfloat16)
        grads_one[layer_idx] = jnp.einsum('bd,bf->df', normed_lo, d_pre, preferred_element_type=jnp.float32)
        if layer_idx > 0:
            d_normed = jnp.einsum('bf,df->bd', d_pre, one_lo[layer_idx], preferred_element_type=jnp.float32)
            d_hidden = d_hidden + inv_rms * (d_normed - normed * jnp.mean(d_normed * normed, axis=-1, keepdims=True))
    return grads_one, grads_two


def solution(mesh):
    n_rows = mesh.shape['row']
    n_cols = mesh.shape['col']
    from_col_prev = [(i, (i + 1) % n_cols) for i in range(n_cols)]
    from_col_next = [(i, (i - 1) % n_cols) for i in range(n_cols)]
    from_row_prev = [(i, (i + 1) % n_rows) for i in range(n_rows)]
    from_row_next = [(i, (i - 1) % n_rows) for i in range(n_rows)]

    def device_fn(w_one, w_two, inputs, targets):
        n_layers = w_one.shape[2]
        one_list = [w_one[0, 0, k] for k in range(n_layers)]
        two_list = [w_two[0, 0, k] for k in range(n_layers)]
        for step_idx in range(inputs.shape[2]):
            grads_one, grads_two = local_grads(one_list, two_list, inputs[0, 0, step_idx], targets[0, 0, step_idx])
            upd_vals = [w - LEARN_RATE * g for w, g in zip(one_list + two_list, grads_one + grads_two)]
            wire_vals = [v.astype(jnp.bfloat16) for v in upd_vals]
            recv_cp = lax.ppermute(wire_vals, 'col', from_col_prev)
            recv_cn = lax.ppermute(wire_vals, 'col', from_col_next)
            recv_rp = lax.ppermute(wire_vals, 'row', from_row_prev)
            recv_rn = lax.ppermute(wire_vals, 'row', from_row_next)
            mixed_vals = [(own_val + cp_val.astype(jnp.float32) + cn_val.astype(jnp.float32) + rp_val.astype(jnp.float32) + rn_val.astype(jnp.float32)) / 5.0 for own_val, cp_val, cn_val, rp_val, rn_val in zip(upd_vals, recv_cp, recv_cn, recv_rp, recv_rn)]
            one_list = mixed_vals[:n_layers]
            two_list = mixed_vals[n_layers:]
        return jnp.stack(one_list)[None, None], jnp.stack(two_list)[None, None]

    grid_spec = P('row', 'col')
    return jax.shard_map(device_fn, mesh=mesh, in_specs=(grid_spec, grid_spec, grid_spec, grid_spec), out_specs=(grid_spec, grid_spec), check_vma=False)
```

profile of v0, /device:TPU:0, one launch (start us, length us, event | category | flops | bytes accessed | tf_op | source)
XLA Modules:
  0.0 1053.9 jit_solution(7644288150337372738)
XLA Ops:
  33.0 10.4 fusion.162
  74.3 16.0 %fusion.12 = bf16[2048,1536]{1,0:T(8,128)(2,1)} fusion(f32[2048,1536]{1,0:T(8,128)} %fusion.280, f32[1,1,4,1536,384]{4,3,2,1,0:T(8,128)} %param.5, bf16[2048,384]{0,1:T(8,128)(2,1)} %fusion.165, bf16[1,1,1,2048,384]{3,4,2,1,0:T(8,128)(2,1)} %copy.19), kind=kOutput, calls=%fused_computation.36 | convolution fusion | flops 2479620096 | bytes 23199744 | tf_op jit(solution)/shard_map/bd,fd->bf/dot_general | solution.py:46
  97.6 15.1 %fusion.17 = bf16[2048,1536]{1,0:T(8,128)(2,1)} fusion(f32[2048,1536]{1,0:T(8,128)} %fusion.283, f32[2048,384]{0,1:T(8,128)S(1)} %fusion.150, f32[1,1,4,1536,384]{4,3,2,1,0:T(8,128)} %param.5), kind=kOutput, calls=%fused_computation.41 | convolution fusion | flops 2476474368 | bytes 23199744 | tf_op jit(solution)/shard_map/bd,fd->bf/dot_general | solution.py:46
  119.5 13.6 %fusion.22 = bf16[2048,1536]{1,0:T(8,128)(2,1)} fusion(f32[2048,1536]{1,0:T(8,128)S(1)} %fusion.286, f32[2048,384]{0,1:T(8,128)S(1)} %fusion.154, f32[1,1,4,1536,384]{4,3,2,1,0:T(8,128)} %param.5), kind=kOutput, calls=%fused_computation.46 | convolution fusion | flops 2476474368 | bytes 23199744 | tf_op jit(solution)/shard_map/bd,fd->bf/dot_general | solution.py:46
  140.1 15.7 %fusion.376 = (bf16[384,1536]{1,0:T(8,128)(2,1)}, f32[384,1536]{1,0:T(8,128)}) fusion(f32[2048,1536]{1,0:T(8,128)} %copy-done.10, bf16[2048,384]{0,1:T(8,128)(2,1)S(1)} %fusion.159, f32[1,1,4,1536,384]{4,3,2,1,0:T(8,128)} %param.5, bf16[1,1,1,2048,384]{3,4,2,1,0:T(8,128)(2,1)S(1)} %copy-done.12, f32[2048]{0:T(1024)S(1)} %copy-done.105, ...), kind=kOutput, calls=%fused_computation.491 | convolution fusion | flops 4895735808 | bytes 22814720 | tf_op jit(solution)/shard_map/bd,bf->df/dot_general | solution.py:48
  253.7 28.1 %collective-permute-done.8 = bf16[384,1536]{1,0:T(8,128)(2,1)S(1)} collective-permute-done((bf16[384,1536]{1,0:T(8,128)(2,1)}, bf16[384,1536]{1,0:T(8,128)(2,1)S(1)}, u32[]{:S(2)}, u32[]{:S(2)}) %collective-permute-start.8) | collective-permute-done | bytes 1179680 | tf_op jit(solution)/shard_map/ppermute | solution.py:73
  288.2 20.7 %collective-permute-done.11 = bf16[1536,384]{1,0:T(8,128)(2,1)S(1)} collective-permute-done((bf16[1536,384]{1,0:T(8,128)(2,1)}, bf16[1536,384]{1,0:T(8,128)(2,1)S(1)}, u32[]{:S(2)}, u32[]{:S(2)}) %collective-permute-start.11) | collective-permute-done | bytes 1179680 | tf_op jit(solution)/shard_map/ppermute | solution.py:73
  318.3 16.8 %collective-permute-done.14 = bf16[384,1536]{1,0:T(8,128)(2,1)S(1)} collective-permute-done((bf16[384,1536]{1,0:T(8,128)(2,1)}, bf16[384,1536]{1,0:T(8,128)(2,1)S(1)}, u32[]{:S(2)}, u32[]{:S(2)}) %collective-permute-start.14) | collective-permute-done | bytes 1179680 | tf_op jit(solution)/shard_map/ppermute | solution.py:73
  344.4 16.9 %collective-permute-done.17 = bf16[1536,384]{1,0:T(8,128)(2,1)S(1)} collective-permute-done((bf16[1536,384]{1,0:T(8,128)(2,1)}, bf16[1536,384]{1,0:T(8,128)(2,1)S(1)}, u32[]{:S(2)}, u32[]{:S(2)}) %collective-permute-start.17) | collective-permute-done | bytes 1179680 | tf_op jit(solution)/shard_map/ppermute | solution.py:73
  374.6 11.2 %collective-permute-done.20 = bf16[384,1536]{1,0:T(8,128)(2,1)} collective-permute-done((bf16[384,1536]{1,0:T(8,128)(2,1)}, bf16[384,1536]{1,0:T(8,128)(2,1)}, u32[]{:S(2)}, u32[]{:S(2)}) %collective-permute-start.20) | collective-permute-done | bytes 1179680 | tf_op jit(solution)/shard_map/ppermute | solution.py:73
  427.8 14.0 %fusion.40 = bf16[2048,1536]{1,0:T(8,128)(2,1)} fusion(f32[2048,1536]{1,0:T(8,128)} %fusion.271, f32[1536,384]{1,0:T(8,128)} %copy-done.80, bf16[2048,384]{0,1:T(8,128)(2,1)S(1)} %fusion.171, bf16[1,1,1,2048,384]{3,4,2,1,0:T(8,128)(2,1)S(1)} %copy-done.48), kind=kOutput, calls=%fused_computation.64 | convolution fusion | flops 2480209920 | bytes 24379392 | tf_op jit(solution)/shard_map/bd,fd->bf/dot_general | solution.py:46
  454.5 13.2 %fusion.45 = bf16[2048,1536]{1,0:T(8,128)(2,1)} fusion(f32[2048,1536]{1,0:T(8,128)S(1)} %fusion.274, f32[2048,384]{0,1:T(8,128)S(1)} %fusion.137, f32[1536,384]{1,0:T(8,128)} %copy-done.78), kind=kOutput, calls=%fused_computation.69 | convolution fusion | flops 2477064192 | bytes 24379392 | tf_op jit(solution)/shard_map/bd,fd->bf/dot_general | solution.py:46
  481.4 13.2 %fusion.50 = bf16[2048,1536]{1,0:T(8,128)(2,1)} fusion(f32[2048,1536]{1,0:T(8,128)S(1)} %bitcast.166, f32[2048,384]{0,1:T(8,128)S(1)} %fusion.141, f32[1536,384]{1,0:T(8,128)} %copy-done.68), kind=kOutput, calls=%fused_computation.74 | convolution fusion | flops 2477064192 | bytes 24379392 | tf_op jit(solution)/shard_map/bd,fd->bf/dot_general | solution.py:46
  509.3 19.0 %fusion.384 = (bf16[384,1536]{1,0:T(8,128)(2,1)}, f32[384,1536]{1,0:T(8,128)}) fusion(f32[2048,1536]{1,0:T(8,128)} %copy-done.1, bf16[2048,384]{0,1:T(8,128)(2,1)} %copy-done.82, f32[1536,384]{1,0:T(8,128)} %copy-done.55, bf16[1,1,1,2048,384]{3,4,2,1,0:T(8,128)(2,1)S(1)} %copy-done.6, f32[2048]{0:T(1024)S(1)} %copy-done.91, ...), kind=kOutput, calls=%fused_computation.499 | convolution fusion | flops 4901044224 | bytes 27533312 | tf_op jit(solution)/shard_map/bd,bf->df/dot_general | solution.py:48
  564.0 9.8 collective-permute-done.26
  589.5 32.7 %collective-permute-done.32 = bf16[384,1536]{1,0:T(8,128)(2,1)S(1)} collective-permute-done((bf16[384,1536]{1,0:T(8,128)(2,1)}, bf16[384,1536]{1,0:T(8,128)(2,1)S(1)}, u32[]{:S(2)}, u32[]{:S(2)}) %collective-permute-start.32) | collective-permute-done | bytes 1179680 | tf_op jit(solution)/shard_map/ppermute | solution.py:73
  630.1 18.3 %collective-permute-done.35 = bf16[1536,384]{1,0:T(8,128)(2,1)S(1)} collective-permute-done((bf16[1536,384]{1,0:T(8,128)(2,1)}, bf16[1536,384]{1,0:T(8,128)(2,1)S(1)}, u32[]{:S(2)}, u32[]{:S(2)}) %collective-permute-start.35) | collective-permute-done | bytes 1179680 | tf_op jit(solution)/shard_map/ppermute | solution.py:73
  658.3 16.2 %collective-permute-done.38 = bf16[384,1536]{1,0:T(8,128)(2,1)S(1)} collective-permute-done((bf16[384,1536]{1,0:T(8,128)(2,1)}, bf16[384,1536]{1,0:T(8,128)(2,1)S(1)}, u32[]{:S(2)}, u32[]{:S(2)}) %collective-permute-start.38) | collective-permute-done | bytes 1179680 | tf_op jit(solution)/shard_map/ppermute | solution.py:73
  684.0 16.6 %collective-permute-done.41 = bf16[1536,384]{1,0:T(8,128)(2,1)S(1)} collective-permute-done((bf16[1536,384]{1,0:T(8,128)(2,1)}, bf16[1536,384]{1,0:T(8,128)(2,1)S(1)}, u32[]{:S(2)}, u32[]{:S(2)}) %collective-permute-start.41) | collective-permute-done | bytes 1179680 | tf_op jit(solution)/shard_map/ppermute | solution.py:73
  723.8 10.1 collective-permute-done.43
  756.5 9.8 fusion.398
  766.3 14.1 %fusion.68 = bf16[2048,1536]{1,0:T(8,128)(2,1)} fusion(f32[2048,1536]{1,0:T(8,128)} %fusion.262, f32[1536,384]{1,0:T(8,128)} %copy-done.81, bf16[2048,384]{0,1:T(8,128)(2,1)S(1)} %fusion.177, bf16[1,1,1,2048,384]{3,4,2,1,0:T(8,128)(2,1)S(1)} %copy-done.47), kind=kOutput, calls=%fused_computation.92 | convolution fusion | flops 2480209920 | bytes 24379392 | tf_op jit(solution)/shard_map/bd,fd->bf/dot_general | solution.py:46
  801.8 13.2 %fusion.73 = bf16[2048,1536]{1,0:T(8,128)(2,1)} fusion(f32[2048,1536]{1,0:T(8,128)S(1)} %fusion.265, f32[2048,384]{0,1:T(8,128)S(1)} %fusion.124, f32[1536,384]{1,0:T(8,128)} %copy-done.74), kind=kOutput, calls=%fused_computation.97 | convolution fusion | flops 2477064192 | bytes 24379392 | tf_op jit(solution)/shard_map/bd,fd->bf/dot_general | solution.py:46
  829.1 13.2 %fusion.78 = bf16[2048,1536]{1,0:T(8,128)(2,1)} fusion(f32[2048,1536]{1,0:T(8,128)S(1)} %bitcast.164, f32[2048,384]{0,1:T(8,128)S(1)} %fusion.128, f32[1536,384]{1,0:T(8,128)} %copy-done.65), kind=kOutput, calls=%fused_computation.102 | convolution fusion | flops 2477064192 | bytes 24379392 | tf_op jit(solution)/shard_map/bd,fd->bf/dot_general | solution.py:46
  849.3 19.1 %fusion.395 = (bf16[384,1536]{1,0:T(8,128)(2,1)}, f32[384,1536]{1,0:T(8,128)}) fusion(f32[2048,1536]{1,0:T(8,128)} %copy-done, bf16[2048,384]{0,1:T(8,128)(2,1)} %fusion.133, f32[1536,384]{1,0:T(8,128)} %copy-done.54, bf16[1,1,1,2048,384]{3,4,2,1,0:T(8,128)(2,1)S(1)} %copy-done.4, f32[2048]{0:T(1024)S(1)} %copy-done.89, bf16[384,1536]{1,0:T(8,128)(2,1)} %copy-done.85, ...), kind=kOutput, calls=%fused_computation.508 | convolution fusion | flops 4901044224 | bytes 27533312 | tf_op jit(solution)/shard_map/bd,bf->df/dot_general | solution.py:48
  892.9 14.4 %collective-permute-done.57 = bf16[384,1536]{1,0:T(8,128)(2,1)S(1)} collective-permute-done((bf16[384,1536]{1,0:T(8,128)(2,1)}, bf16[384,1536]{1,0:T(8,128)(2,1)S(1)}, u32[]{:S(2)}, u32[]{:S(2)}) %collective-permute-start.57) | collective-permute-done | bytes 1179680 | tf_op jit(solution)/shard_map/ppermute | solution.py:71
  914.7 17.8 %collective-permute-done.66 = bf16[1536,384]{1,0:T(8,128)(2,1)S(1)} collective-permute-done((bf16[1536,384]{1,0:T(8,128)(2,1)S(1)}, bf16[1536,384]{1,0:T(8,128)(2,1)S(1)}, u32[]{:S(2)}, u32[]{:S(2)}) %collective-permute-start.66) | collective-permute-done | bytes 1179680 | tf_op jit(solution)/shard_map/ppermute | solution.py:71
  938.2 19.6 %collective-permute-done.54 = bf16[384,1536]{1,0:T(8,128)(2,1)S(1)} collective-permute-done((bf16[384,1536]{1,0:T(8,128)(2,1)S(1)}, bf16[384,1536]{1,0:T(8,128)(2,1)S(1)}, u32[]{:S(2)}, u32[]{:S(2)}) %collective-permute-start.54) | collective-permute-done | bytes 1179680 | tf_op jit(solution)/shard_map/ppermute | solution.py:71
  964.1 19.0 %collective-permute-done.63 = bf16[1536,384]{1,0:T(8,128)(2,1)S(1)} collective-permute-done((bf16[1536,384]{1,0:T(8,128)(2,1)S(1)}, bf16[1536,384]{1,0:T(8,128)(2,1)S(1)}, u32[]{:S(2)}, u32[]{:S(2)}) %collective-permute-start.63) | collective-permute-done | bytes 1179680 | tf_op jit(solution)/shard_map/ppermute | solution.py:71
  988.1 20.2 %collective-permute-done.60 = bf16[1536,384]{1,0:T(8,128)(2,1)S(1)} collective-permute-done((bf16[1536,384]{1,0:T(8,128)(2,1)S(1)}, bf16[1536,384]{1,0:T(8,128)(2,1)S(1)}, u32[]{:S(2)}, u32[]{:S(2)}) %collective-permute-start.60) | collective-permute-done | bytes 1179680 | tf_op jit(solution)/shard_map/ppermute | solution.py:71
  1016.5 17.1 %collective-permute-done.48 = bf16[384,1536]{1,0:T(8,128)(2,1)S(1)} collective-permute-done((bf16[384,1536]{1,0:T(8,128)(2,1)S(1)}, bf16[384,1536]{1,0:T(8,128)(2,1)S(1)}, u32[]{:S(2)}, u32[]{:S(2)}) %collective-permute-start.48) | collective-permute-done | bytes 1179680 | tf_op jit(solution)/shard_map/ppermute | solution.py:71
  1036.8 12.1 %collective-permute-done.51 = bf16[384,1536]{1,0:T(8,128)(2,1)S(1)} collective-permute-done((bf16[384,1536]{1,0:T(8,128)(2,1)S(1)}, bf16[384,1536]{1,0:T(8,128)(2,1)S(1)}, u32[]{:S(2)}, u32[]{:S(2)}) %collective-permute-start.51) | collective-permute-done | bytes 1179680 | tf_op jit(solution)/shard_map/ppermute | solution.py:71
  (524 shorter events, 534.0 us)
Async XLA Ops:
  155.8 78.8 %collective-permute-start.2 = (bf16[384,1536]{1,0:T(8,128)(2,1)}, bf16[384,1536]{1,0:T(8,128)(2,1)}, u32[]{:S(2)}, u32[]{:S(2)}) collective-permute-start(bf16[384,1536]{1,0:T(8,128)(2,1)} %get-tuple-element.24), channel_id=1, source_target_pairs={{0,4},{4,0},{1,5},{5,1},{2,6},{6,2},{3,7},{7,3}} | collective-permute-start | bytes 3538952 | tf_op jit(solution)/shard_map/ppermute | solution.py:73
  159.2 75.8 %collective-permute-start.1 = (bf16[384,1536]{1,0:T(8,128)(2,1)}, bf16[384,1536]{1,0:T(8,128)(2,1)}, u32[]{:S(2)}, u32[]{:S(2)}) collective-permute-start(bf16[384,1536]{1,0:T(8,128)(2,1)} %get-tuple-element.24), channel_id=1, source_target_pairs={{0,3},{1,0},{2,1},{3,2},{4,7},{5,4},{6,5},{7,6}} | collective-permute-start | bytes 3538952 | tf_op jit(solution)/shard_map/ppermute | solution.py:72
  169.1 53.0 %collective-permute-start.5 = (bf16[1536,384]{1,0:T(8,128)(2,1)}, bf16[1536,384]{1,0:T(8,128)(2,1)}, u32[]{:S(2)}, u32[]{:S(2)}) collective-permute-start(bf16[1536,384]{1,0:T(8,128)(2,1)} %get-tuple-element.22), channel_id=1, source_target_pairs={{0,4},{4,0},{1,5},{5,1},{2,6},{6,2},{3,7},{7,3}} | collective-permute-start | bytes 3538952 | tf_op jit(solution)/shard_map/ppermute | solution.py:73
  169.7 58.7 %collective-permute-start.4 = (bf16[1536,384]{1,0:T(8,128)(2,1)}, bf16[1536,384]{1,0:T(8,128)(2,1)}, u32[]{:S(2)}, u32[]{:S(2)}) collective-permute-start(bf16[1536,384]{1,0:T(8,128)(2,1)} %get-tuple-element.22), channel_id=1, source_target_pairs={{0,3},{1,0},{2,1},{3,2},{4,7},{5,4},{6,5},{7,6}} | collective-permute-start | bytes 3538952 | tf_op jit(solution)/shard_map/ppermute | solution.py:72
  170.4 59.8 %collective-permute-start.3 = (bf16[1536,384]{1,0:T(8,128)(2,1)}, bf16[1536,384]{1,0:T(8,128)(2,1)}, u32[]{:S(2)}, u32[]{:S(2)}) collective-permute-start(bf16[1536,384]{1,0:T(8,128)(2,1)} %get-tuple-element.22), channel_id=1, source_target_pairs={{0,1},{1,2},{2,3},{3,0},{4,5},{5,6},{6,7},{7,4}} | collective-permute-start | bytes 3538952 | tf_op jit(solution)/shard_map/ppermute | solution.py:71
  228.5 175.5 %collective-permute-start.23 = (bf16[1536,384]{1,0:T(8,128)(2,1)}, bf16[1536,384]{1,0:T(8,128)(2,1)S(1)}, u32[]{:S(2)}, u32[]{:S(2)}) collective-permute-start(bf16[1536,384]{1,0:T(8,128)(2,1)} %get-tuple-element.40), channel_id=1, source_target_pairs={{0,4},{4,0},{1,5},{5,1},{2,6},{6,2},{3,7},{7,3}} | collective-permute-start | bytes 3538952 | tf_op jit(solution)/shard_map/ppermute | solution.py:73
  230.2 173.7 %collective-permute-start.22 = (bf16[1536,384]{1,0:T(8,128)(2,1)}, bf16[1536,384]{1,0:T(8,128)(2,1)S(1)}, u32[]{:S(2)}, u32[]{:S(2)}) collective-permute-start(bf16[1536,384]{1,0:T(8,128)(2,1)} %get-tuple-element.40), channel_id=1, source_target_pairs={{0,3},{1,0},{2,1},{3,2},{4,7},{5,4},{6,5},{7,6}} | collective-permute-start | bytes 3538952 | tf_op jit(solution)/shard_map/ppermute | solution.py:72
  234.6 47.1 %collective-permute-start.8 = (bf16[384,1536]{1,0:T(8,128)(2,1)}, bf16[384,1536]{1,0:T(8,128)(2,1)S(1)}, u32[]{:S(2)}, u32[]{:S(2)}) collective-permute-start(bf16[384,1536]{1,0:T(8,128)(2,1)} %get-tuple-element.30), channel_id=1, source_target_pairs={{0,4},{4,0},{1,5},{5,1},{2,6},{6,2},{3,7},{7,3}} | collective-permute-start | bytes 3538952 | tf_op jit(solution)/shard_map/ppermute | solution.py:73
  235.0 48.5 %collective-permute-start.7 = (bf16[384,1536]{1,0:T(8,128)(2,1)}, bf16[384,1536]{1,0:T(8,128)(2,1)S(1)}, u32[]{:S(2)}, u32[]{:S(2)}) collective-permute-start(bf16[384,1536]{1,0:T(8,128)(2,1)} %get-tuple-element.30), channel_id=1, source_target_pairs={{0,3},{1,0},{2,1},{3,2},{4,7},{5,4},{6,5},{7,6}} | collective-permute-start | bytes 3538952 | tf_op jit(solution)/shard_map/ppermute | solution.py:72
  242.4 41.1 %collective-permute-start.6 = (bf16[384,1536]{1,0:T(8,128)(2,1)}, bf16[384,1536]{1,0:T(8,128)(2,1)S(1)}, u32[]{:S(2)}, u32[]{:S(2)}) collective-permute-start(bf16[384,1536]{1,0:T(8,128)(2,1)} %get-tuple-element.30), channel_id=1, source_target_pairs={{0,1},{1,2},{2,3},{3,0},{4,5},{5,6},{6,7},{7,4}} | collective-permute-start | bytes 3538952 | tf_op jit(solution)/shard_map/ppermute | solution.py:71
  509.3 50.2 %collective-permute-start.27 = (bf16[1536,384]{1,0:T(8,128)(2,1)}, bf16[1536,384]{1,0:T(8,128)(2,1)}, u32[]{:S(2)}, u32[]{:S(2)}) collective-permute-start(bf16[1536,384]{1,0:T(8,128)(2,1)} %get-tuple-element.50), channel_id=1, source_target_pairs={{0,1},{1,2},{2,3},{3,0},{4,5},{5,6},{6,7},{7,4}} | collective-permute-start | bytes 3538952 | tf_op jit(solution)/shard_map/ppermute | solution.py:71
  557.2 185.5 %collective-permute-start.47 = (bf16[1536,384]{1,0:T(8,128)(2,1)}, bf16[1536,384]{1,0:T(8,128)(2,1)S(1)}, u32[]{:S(2)}, u32[]{:S(2)}) collective-permute-start(bf16[1536,384]{1,0:T(8,128)(2,1)} %get-tuple-element.68), channel_id=1, source_target_pairs={{0,4},{4,0},{1,5},{5,1},{2,6},{6,2},{3,7},{7,3}} | collective-permute-start | bytes 3538952 | tf_op jit(solution)/shard_map/ppermute | solution.py:73
  559.5 183.2 %collective-permute-start.46 = (bf16[1536,384]{1,0:T(8,128)(2,1)}, bf16[1536,384]{1,0:T(8,128)(2,1)}, u32[]{:S(2)}, u32[]{:S(2)}) collective-permute-start(bf16[1536,384]{1,0:T(8,128)(2,1)} %get-tuple-element.68), channel_id=1, source_target_pairs={{0,3},{1,0},{2,1},{3,2},{4,7},{5,4},{6,5},{7,6}} | collective-permute-start | bytes 3538952 | tf_op jit(solution)/shard_map/ppermute | solution.py:72
  573.8 48.4 %collective-permute-start.32 = (bf16[384,1536]{1,0:T(8,128)(2,1)}, bf16[384,1536]{1,0:T(8,128)(2,1)S(1)}, u32[]{:S(2)}, u32[]{:S(2)}) collective-permute-start(bf16[384,1536]{1,0:T(8,128)(2,1)} %get-tuple-element.58), channel_id=1, source_target_pairs={{0,4},{4,0},{1,5},{5,1},{2,6},{6,2},{3,7},{7,3}} | collective-permute-start | bytes 3538952 | tf_op jit(solution)/shard_map/ppermute | solution.py:73
  577.5 46.1 %collective-permute-start.31 = (bf16[384,1536]{1,0:T(8,128)(2,1)}, bf16[384,1536]{1,0:T(8,128)(2,1)}, u32[]{:S(2)}, u32[]{:S(2)}) collective-permute-start(bf16[384,1536]{1,0:T(8,128)(2,1)} %get-tuple-element.58), channel_id=1, source_target_pairs={{0,3},{1,0},{2,1},{3,2},{4,7},{5,4},{6,5},{7,6}} | collective-permute-start | bytes 3538952 | tf_op jit(solution)/shard_map/ppermute | solution.py:72
  579.8 43.9 %collective-permute-start.30 = (bf16[384,1536]{1,0:T(8,128)(2,1)}, bf16[384,1536]{1,0:T(8,128)(2,1)}, u32[]{:S(2)}, u32[]{:S(2)}) collective-permute-start(bf16[384,1536]{1,0:T(8,128)(2,1)} %get-tuple-element.58), channel_id=1, source_target_pairs={{0,1},{1,2},{2,3},{3,0},{4,5},{5,6},{6,7},{7,4}} | collective-permute-start | bytes 3538952 | tf_op jit(solution)/shard_map/ppermute | solution.py:71
  780.5 101.1 %collective-permute-start.71 = (bf16[1536,384]{1,0:T(8,128)(2,1)}, bf16[1536,384]{1,0:T(8,128)(2,1)}, u32[]{:S(2)}, u32[]{:S(2)}) collective-permute-start(bf16[1536,384]{1,0:T(8,128)(2,1)} %get-tuple-element.84), channel_id=1, source_target_pairs={{0,4},{4,0},{1,5},{5,1},{2,6},{6,2},{3,7},{7,3}} | collective-permute-start | bytes 3538952 | tf_op jit(solution)/shard_map/ppermute | solution.py:73
  781.1 100.5 %collective-permute-start.70 = (bf16[1536,384]{1,0:T(8,128)(2,1)}, bf16[1536,384]{1,0:T(8,128)(2,1)}, u32[]{:S(2)}, u32[]{:S(2)}) collective-permute-start(bf16[1536,384]{1,0:T(8,128)(2,1)} %get-tuple-element.84), channel_id=1, source_target_pairs={{0,3},{1,0},{2,1},{3,2},{4,7},{5,4},{6,5},{7,6}} | collective-permute-start | bytes 3538952 | tf_op jit(solution)/shard_map/ppermute | solution.py:72
  781.1 101.5 %collective-permute-start.69 = (bf16[1536,384]{1,0:T(8,128)(2,1)}, bf16[1536,384]{1,0:T(8,128)(2,1)}, u32[]{:S(2)}, u32[]{:S(2)}) collective-permute-start(bf16[1536,384]{1,0:T(8,128)(2,1)} %get-tuple-element.84), channel_id=1, source_target_pairs={{0,1},{1,2},{2,3},{3,0},{4,5},{5,6},{6,7},{7,4}} | collective-permute-start | bytes 3538952 | tf_op jit(solution)/shard_map/ppermute | solution.py:71
  791.4 97.5 %collective-permute-start.59 = (bf16[384,1536]{1,0:T(8,128)(2,1)}, bf16[384,1536]{1,0:T(8,128)(2,1)}, u32[]{:S(2)}, u32[]{:S(2)}) collective-permute-start(bf16[384,1536]{1,0:T(8,128)(2,1)} %get-tuple-element.70), channel_id=1, source_target_pairs={{0,4},{4,0},{1,5},{5,1},{2,6},{6,2},{3,7},{7,3}} | collective-permute-start | bytes 3538952 | tf_op jit(solution)/shard_map/ppermute | solution.py:73
  792.3 96.8 %collective-permute-start.58 = (bf16[384,1536]{1,0:T(8,128)(2,1)}, bf16[384,1536]{1,0:T(8,128)(2,1)}, u32[]{:S(2)}, u32[]{:S(2)}) collective-permute-start(bf16[384,1536]{1,0:T(8,128)(2,1)} %get-tuple-element.70), channel_id=1, source_target_pairs={{0,3},{1,0},{2,1},{3,2},{4,7},{5,4},{6,5},{7,6}} | collective-permute-start | bytes 3538952 | tf_op jit(solution)/shard_map/ppermute | solution.py:72
  889.0 43.5 %collective-permute-start.66 = (bf16[1536,384]{1,0:T(8,128)(2,1)S(1)}, bf16[1536,384]{1,0:T(8,128)(2,1)S(1)}, u32[]{:S(2)}, u32[]{:S(2)}) collective-permute-start(bf16[1536,384]{1,0:T(8,128)(2,1)S(1)} %copy-done.109), channel_id=1, source_target_pairs={{0,1},{1,2},{2,3},{3,0},{4,5},{5,6},{6,7},{7,4}} | collective-permute-start | bytes 3538952 | tf_op jit(solution)/shard_map/ppermute | solution.py:71
  889.1 46.0 %collective-permute-start.56 = (bf16[384,1536]{1,0:T(8,128)(2,1)S(1)}, bf16[384,1536]{1,0:T(8,128)(2,1)S(1)}, u32[]{:S(2)}, u32[]{:S(2)}) collective-permute-start(bf16[384,1536]{1,0:T(8,128)(2,1)S(1)} %get-tuple-element.74), channel_id=1, source_target_pairs={{0,4},{4,0},{1,5},{5,1},{2,6},{6,2},{3,7},{7,3}} | collective-permute-start | bytes 3538952 | tf_op jit(solution)/shard_map/ppermute | solution.py:73
  909.8 48.0 %collective-permute-start.54 = (bf16[384,1536]{1,0:T(8,128)(2,1)S(1)}, bf16[384,1536]{1,0:T(8,128)(2,1)S(1)}, u32[]{:S(2)}, u32[]{:S(2)}) collective-permute-start(bf16[384,1536]{1,0:T(8,128)(2,1)S(1)} %get-tuple-element.74), channel_id=1, source_target_pairs={{0,1},{1,2},{2,3},{3,0},{4,5},{5,6},{6,7},{7,4}} | collective-permute-start | bytes 3538952 | tf_op jit(solution)/shard_map/ppermute | solution.py:71
  911.4 49.0 %collective-permute-start.65 = (bf16[1536,384]{1,0:T(8,128)(2,1)S(1)}, bf16[1536,384]{1,0:T(8,128)(2,1)S(1)}, u32[]{:S(2)}, u32[]{:S(2)}) collective-permute-start(bf16[1536,384]{1,0:T(8,128)(2,1)S(1)} %copy-done.108), channel_id=1, source_target_pairs={{0,4},{4,0},{1,5},{5,1},{2,6},{6,2},{3,7},{7,3}} | collective-permute-start | bytes 3538952 | tf_op jit(solution)/shard_map/ppermute | solution.py:73
  935.0 48.0 %collective-permute-start.63 = (bf16[1536,384]{1,0:T(8,128)(2,1)S(1)}, bf16[1536,384]{1,0:T(8,128)(2,1)S(1)}, u32[]{:S(2)}, u32[]{:S(2)}) collective-permute-start(bf16[1536,384]{1,0:T(8,128)(2,1)S(1)} %copy-done.108), channel_id=1, source_target_pairs={{0,1},{1,2},{2,3},{3,0},{4,5},{5,6},{6,7},{7,4}} | collective-permute-start | bytes 3538952 | tf_op jit(solution)/shard_map/ppermute | solution.py:71
  937.3 48.3 %collective-permute-start.62 = (bf16[1536,384]{1,0:T(8,128)(2,1)S(1)}, bf16[1536,384]{1,0:T(8,128)(2,1)S(1)}, u32[]{:S(2)}, u32[]{:S(2)}) collective-permute-start(bf16[1536,384]{1,0:T(8,128)(2,1)S(1)} %get-tuple-element.90), channel_id=1, source_target_pairs={{0,4},{4,0},{1,5},{5,1},{2,6},{6,2},{3,7},{7,3}} | collective-permute-start | bytes 3538952 | tf_op jit(solution)/shard_map/ppermute | solution.py:73
  960.3 48.0 %collective-permute-start.60 = (bf16[1536,384]{1,0:T(8,128)(2,1)S(1)}, bf16[1536,384]{1,0:T(8,128)(2,1)S(1)}, u32[]{:S(2)}, u32[]{:S(2)}) collective-permute-start(bf16[1536,384]{1,0:T(8,128)(2,1)S(1)} %get-tuple-element.90), channel_id=1, source_target_pairs={{0,1},{1,2},{2,3},{3,0},{4,5},{5,6},{6,7},{7,4}} | collective-permute-start | bytes 3538952 | tf_op jit(solution)/shard_map/ppermute | solution.py:71
  963.2 47.7 %collective-permute-start.50 = (bf16[384,1536]{1,0:T(8,128)(2,1)S(1)}, bf16[384,1536]{1,0:T(8,128)(2,1)S(1)}, u32[]{:S(2)}, u32[]{:S(2)}) collective-permute-start(bf16[384,1536]{1,0:T(8,128)(2,1)S(1)} %copy-done.107), channel_id=1, source_target_pairs={{0,4},{4,0},{1,5},{5,1},{2,6},{6,2},{3,7},{7,3}} | collective-permute-start | bytes 3538952 | tf_op jit(solution)/shard_map/ppermute | solution.py:73
  985.6 48.0 %collective-permute-start.48 = (bf16[384,1536]{1,0:T(8,128)(2,1)S(1)}, bf16[384,1536]{1,0:T(8,128)(2,1)S(1)}, u32[]{:S(2)}, u32[]{:S(2)}) collective-permute-start(bf16[384,1536]{1,0:T(8,128)(2,1)S(1)} %copy-done.107), channel_id=1, source_target_pairs={{0,1},{1,2},{2,3},{3,0},{4,5},{5,6},{6,7},{7,4}} | collective-permute-start | bytes 3538952 | tf_op jit(solution)/shard_map/ppermute | solution.py:71
  987.2 49.0 %collective-permute-start.53 = (bf16[384,1536]{1,0:T(8,128)(2,1)S(1)}, bf16[384,1536]{1,0:T(8,128)(2,1)S(1)}, u32[]{:S(2)}, u32[]{:S(2)}) collective-permute-start(bf16[384,1536]{1,0:T(8,128)(2,1)S(1)} %get-tuple-element.78), channel_id=1, source_target_pairs={{0,4},{4,0},{1,5},{5,1},{2,6},{6,2},{3,7},{7,3}} | collective-permute-start | bytes 3538952 | tf_op jit(solution)/shard_map/ppermute | solution.py:73
  1010.9 38.0 %collective-permute-start.51 = (bf16[384,1536]{1,0:T(8,128)(2,1)S(1)}, bf16[384,1536]{1,0:T(8,128)(2,1)S(1)}, u32[]{:S(2)}, u32[]{:S(2)}) collective-permute-start(bf16[384,1536]{1,0:T(8,128)(2,1)S(1)} %get-tuple-element.78), channel_id=1, source_target_pairs={{0,1},{1,2},{2,3},{3,0},{4,5},{5,6},{6,7},{7,4}} | collective-permute-start | bytes 3538952 | tf_op jit(solution)/shard_map/ppermute | solution.py:71
  (176 other events, 3336.4 us)
where the time goes:
time: 1060 us; the launch traced here: 1050 us
  matrix products  523 us (49%)
  waiting for transfers between devices  386 us (36%)
  starting transfers between devices  64.5 us (6%)
  other arithmetic  49.2 us (5%)
  local copies, waits for them, and re-layouts  29.1 us (3%)
    ppermute x24, waiting for transfers between devices, device_fn(): recv_rp = lax.ppermute(wire_vals, 'row', from_row_prev)  210 us
    ppermute x24, waiting for transfers between devices, device_fn(): recv_cp = lax.ppermute(wire_vals, 'col', from_col_prev)  150 us
    dot_general x9, matrix products, local_grads(): jnp.einsum('bd,fd->bf', d_lo, two_lo[layer_idx], preferred_element_type=j...  125 us
    dot_general x12, matrix products, local_grads(): jnp.einsum('bd,bf->df', normed_lo, d_pre, preferred_element_type=jnp.floa...  111 us
    dot_general x12, matrix products, local_grads(): jnp.einsum('bf,bd->fd', act_lo, d_lo, preferred_element_type=jnp.float32)  90.4 us
    dot_general x12, matrix products, local_grads(): jnp.dot(act_lo, two_lo[layer_idx], preferred_element_type=jnp.float32)  88.6 us
    dot_general x12, matrix products, local_grads(): jnp.dot(normed_lo, one_lo[layer_idx], preferred_element_type=jnp.float32)  59.4 us
    dot_general x9, matrix products, local_grads(): jnp.einsum('bf,df->bd', d_pre, one_lo[layer_idx], preferred_element_type=...  47.9 us
  transfers between devices with their start and end apart: 72, of which 37 were waited for; matrix products, arithmetic and copies ran while one was open for 29% of the time, Pallas kernels for 0%

commit v1 on v0

v1 whole, which is shorter than its diff:
```python
import functools

import jax
import jax.numpy as jnp
from jax import lax
from jax.experimental import pallas as pl
from jax.experimental.pallas import tpu as pltpu
from jax.sharding import PartitionSpec as P

LEARN_RATE = 1.5
NORM_EPS = 1e-6
GELU_C = 0.7978845608028654
GELU_K = 0.044715

MESH = pl.DeviceIdType.MESH
F32 = jnp.float32
BF16 = jnp.bfloat16
CHUNKS = 3
TILE = 512


def matmul(lhs, rhs):
    return jnp.dot(lhs, rhs, preferred_element_type=F32)


def matmul_t(lhs, rhs):
    return lax.dot_general(lhs, rhs, (((1,), (1,)), ((), ())), preferred_element_type=F32)


def gelu_half(pre_act):
    sq = pre_act * pre_act
    t = jnp.tanh(pre_act * (GELU_C + (GELU_C * GELU_K) * sq))
    return sq, t, 0.5 + 0.5 * t


def inv_rms_of(hid_f):
    return lax.rsqrt(jnp.mean(hid_f * hid_f, axis=-1, keepdims=True) + NORM_EPS)


def kernel(dims, w1_hbm, w2_hbm, x_hbm, tgt_hbm, o1_hbm, o2_hbm, r1_hbm, r2_hbm,
           m1, m2, l1, l2, hs, err, acc, tgt, act, dpre, nrm, err_lo, nrm_t, err_t, st1, st2,
           load_sem, data_sem, stage_sem, out_sem, send_sem, recv_sem):
    n_rows, n_cols, n_steps, n_layers, batch, d_model, d_ff = dims
    f_blk = d_ff // CHUNKS
    n_blk = n_layers * CHUNKS
    n_tiles = batch // TILE
    row, col = lax.axis_index("row"), lax.axis_index("col")
    peers = ((row, lax.rem(col + 1, n_cols)), (row, lax.rem(col + n_cols - 1, n_cols)), (n_rows - 1 - row, col))

    def cols_of(blk):
        return pl.ds(pl.multiple_of(lax.rem(blk, CHUNKS) * f_blk, f_blk), f_blk)

    def load_copies(blk):
        layer = lax.div(blk, CHUNKS)
        return (pltpu.make_async_copy(w1_hbm.at[layer, :, cols_of(blk)], m1.at[blk], load_sem.at[blk, 0]),
                pltpu.make_async_copy(w2_hbm.at[layer, cols_of(blk), :], m2.at[blk], load_sem.at[blk, 1]))

    def out_copies(blk):
        layer = lax.div(blk, CHUNKS)
        return (pltpu.make_async_copy(m1.at[blk], o1_hbm.at[layer, :, cols_of(blk)], out_sem.at[blk, 0]),
                pltpu.make_async_copy(m2.at[blk], o2_hbm.at[layer, cols_of(blk), :], out_sem.at[blk, 1]))

    def data_copies(step):
        return (pltpu.make_async_copy(x_hbm.at[step], hs.at[0], data_sem.at[0]),
                pltpu.make_async_copy(tgt_hbm.at[step], tgt, data_sem.at[1]))

    def sends(step, blk):
        out = []
        for slot, peer in enumerate(peers):
            for mat, (src, dst) in enumerate(((l2, r2_hbm), (l1, r1_hbm))):
                out.append(pltpu.make_async_remote_copy(
                    src_ref=src.at[blk], dst_ref=dst.at[step, slot, blk],
                    send_sem=send_sem.at[blk, mat, slot], recv_sem=recv_sem.at[step, blk, mat, slot],
                    device_id=peer, device_id_type=MESH))
        return out

    def start_sends(step, blk):
        for cp in sends(step, blk):
            cp.start()

    def sent_early(blk):
        layer, chunk = lax.div(blk, CHUNKS), lax.rem(blk, CHUNKS)
        head = jnp.logical_and(chunk == 0, layer > 0)
        return jnp.logical_or(head, blk == n_blk - 2)

    def tile_rows(i):
        return pl.ds(pl.multiple_of(i * TILE, TILE), TILE)

    def mix(step, blk):
        for cp in sends(step, blk):
            cp.wait_recv()
        stage = []
        for slot in range(3):
            stage.append(pltpu.make_async_copy(r1_hbm.at[step, slot, blk], st1.at[slot], stage_sem.at[0, slot]))
            stage.append(pltpu.make_async_copy(r2_hbm.at[step, slot, blk], st2.at[slot], stage_sem.at[1, slot]))
        for cp in stage:
            cp.start()
        for cp in sends(step, blk):
            cp.wait_send()
        for cp in stage:
            cp.wait()
        for own, lo, st in ((m1, l1, st1), (m2, l2, st2)):
            other = st[2].astype(F32)
            new = (own[blk] + st[0].astype(F32) + st[1].astype(F32) + other + other) * 0.2
            own[blk] = new
            lo[blk] = new.astype(BF16)

    barrier = pltpu.get_barrier_semaphore()
    for peer in peers:
        pl.semaphore_signal(barrier, inc=1, device_id=peer, device_id_type=MESH)
    for cp in data_copies(0):
        cp.start()

    @pl.loop(0, n_blk)
    def _(blk):
        for cp in load_copies(blk):
            cp.start()

    pl.semaphore_wait(barrier, 3)

    @pl.loop(0, n_steps)
    def _(step):
        for cp in data_copies(step):
            cp.wait()

        @pl.loop(0, n_blk)
        def _(blk):
            layer, chunk = lax.div(blk, CHUNKS), lax.rem(blk, CHUNKS)

            @pl.when(chunk == 0)
            def _():
                @pl.loop(0, n_tiles)
                def _(i):
                    rows = tile_rows(i)
                    hid_f = hs[layer, rows, :].astype(F32)
                    nrm[rows, :] = (hid_f * inv_rms_of(hid_f)).astype(BF16)
                    acc[rows, :] = hid_f

            @pl.when(step == 0)
            def _():
                for cp in load_copies(blk):
                    cp.wait()
                l1[blk] = m1[blk].astype(BF16)
                l2[blk] = m2[blk].astype(BF16)

            @pl.when(step > 0)
            def _():
                mix(step - 1, blk)

            @pl.loop(0, n_tiles)
            def _(i):
                rows = tile_rows(i)
                pre = matmul(nrm[rows, :], l1[blk])
                _, _, half = gelu_half(pre)
                acc[rows, :] += matmul((pre * half).astype(BF16), l2[blk])

            @pl.when(jnp.logical_and(chunk == CHUNKS - 1, layer < n_layers - 1))
            def _():
                @pl.loop(0, n_tiles)
                def _(i):
                    rows = tile_rows(i)
                    hs[lax.min(layer + 1, n_layers - 1), rows, :] = acc[rows, :].astype(BF16)

        @pl.loop(0, n_tiles)
        def _(i):
            rows = tile_rows(i)
            hid = acc[rows, :].astype(BF16).astype(F32)
            err[rows, :] = (2.0 / (batch * d_model)) * (hid - tgt[rows, :].astype(F32))

        @pl.loop(0, n_blk)
        def _(k):
            layer, chunk = n_layers - 1 - lax.div(k, CHUNKS), lax.rem(k, CHUNKS)
            blk = layer * CHUNKS + chunk

            @pl.when(chunk == 0)
            def _():
                @pl.loop(0, n_tiles)
                def _(i):
                    rows = tile_rows(i)
                    hid_f = hs[layer, rows, :].astype(F32)
                    n_f = hid_f * inv_rms_of(hid_f)
                    nrm[rows, :] = n_f.astype(BF16)
                    nrm_t[:, rows] = n_f.T.astype(BF16)
                    e_f = err[rows, :]
                    err_lo[rows, :] = e_f.astype(BF16)
                    err_t[:, rows] = e_f.T.astype(BF16)
                    acc[rows, :] = jnp.zeros((TILE, d_model), F32)

            @pl.loop(0, n_tiles)
            def _(i):
                rows = tile_rows(i)
                pre = matmul(nrm[rows, :], l1[blk])
                sq, t, half = gelu_half(pre)
                act[rows, :] = (pre * half).astype(BF16)
                slope = half + ((half * (1.0 - t)) * pre) * (GELU_C + (3.0 * GELU_C * GELU_K) * sq)
                d_pre = (matmul_t(err_lo[rows, :], l2[blk]) * slope).astype(BF16)
                dpre[rows, :] = d_pre
                acc[rows, :] += matmul_t(d_pre, l1[blk])

            grad_two = matmul(err_t[...], act[...]).T
            upd_two = m2[blk] - LEARN_RATE * grad_two
            m2[blk] = upd_two
            l2[blk] = upd_two.astype(BF16)
            grad_one = matmul(nrm_t[...], dpre[...])
            upd_one = m1[blk] - LEARN_RATE * grad_one
            m1[blk] = upd_one
            l1[blk] = upd_one.astype(BF16)

            @pl.when(sent_early(blk))
            def _():
                start_sends(step, blk)

            @pl.when(jnp.logical_and(chunk == CHUNKS - 1, layer > 0))
            def _():
                @pl.loop(0, n_tiles)
                def _(i):
                    rows = tile_rows(i)
                    hid_f = hs[layer, rows, :].astype(F32)
                    inv = inv_rms_of(hid_f)
                    n_f = hid_f * inv
                    d_n = acc[rows, :]
                    err[rows, :] += inv * (d_n - n_f * jnp.mean(d_n * n_f, axis=-1, keepdims=True))

        @pl.loop(0, n_blk)
        def _(blk):
            @pl.when(jnp.logical_not(sent_early(blk)))
            def _():
                start_sends(step, blk)

        @pl.when(step < n_steps - 1)
        def _():
            for cp in data_copies(lax.min(step + 1, n_steps - 1)):
                cp.start()

    for early in (True, False):
        @pl.loop(0, n_blk)
        def _(blk):
            turn = sent_early(blk) if early else jnp.logical_not(sent_early(blk))

            @pl.when(turn)
            def _():
                mix(n_steps - 1, blk)
                for cp in out_copies(blk):
                    cp.start()

    @pl.loop(0, n_blk)
    def _(blk):
        for cp in out_copies(blk):
            cp.wait()


def solution(mesh):
    n_rows = mesh.shape['row']
    n_cols = mesh.shape['col']

    def device_fn(w_one, w_two, inputs, targets):
        n_layers, d_model, d_ff = w_one.shape[2:]
        n_steps, batch = inputs.shape[2:4]
        f_blk = d_ff // CHUNKS
        n_blk = n_layers * CHUNKS
        dims = (n_rows, n_cols, n_steps, n_layers, batch, d_model, d_ff)
        any_spec = pl.BlockSpec(memory_space=pl.ANY)
        out = pl.pallas_call(
            functools.partial(kernel, dims),
            out_shape=(
                jax.ShapeDtypeStruct((n_layers, d_model, d_ff), F32),
                jax.ShapeDtypeStruct((n_layers, d_ff, d_model), F32),
                jax.ShapeDtypeStruct((n_steps, 3, n_blk, d_model, f_blk), BF16),
                jax.ShapeDtypeStruct((n_steps, 3, n_blk, f_blk, d_model), BF16),
            ),
            in_specs=[any_spec] * 4,
            out_specs=(any_spec,) * 4,
            scratch_shapes=[
                pltpu.VMEM((n_blk, d_model, f_blk), F32),
                pltpu.VMEM((n_blk, f_blk, d_model), F32),
                pltpu.VMEM((n_blk, d_model, f_blk), BF16),
                pltpu.VMEM((n_blk, f_blk, d_model), BF16),
                pltpu.VMEM((n_layers, batch, d_model), BF16),
                pltpu.VMEM((batch, d_model), F32),
                pltpu.VMEM((batch, d_model), F32),
                pltpu.VMEM((batch, d_model), BF16),
                pltpu.VMEM((batch, f_blk), BF16),
                pltpu.VMEM((batch, f_blk), BF16),
                pltpu.VMEM((batch, d_model), BF16),
                pltpu.VMEM((batch, d_model), BF16),
                pltpu.VMEM((d_model, batch), BF16),
                pltpu.VMEM((d_model, batch), BF16),
                pltpu.VMEM((3, d_model, f_blk), BF16),
                pltpu.VMEM((3, f_blk, d_model), BF16),
                pltpu.SemaphoreType.DMA((n_blk, 2)),
                pltpu.SemaphoreType.DMA((2,)),
                pltpu.SemaphoreType.DMA((2, 3)),
                pltpu.SemaphoreType.DMA((n_blk, 2)),
                pltpu.SemaphoreType.DMA((n_blk, 2, 3)),
                pltpu.SemaphoreType.DMA((n_steps, n_blk, 2, 3)),
            ],
            compiler_params=pltpu.CompilerParams(
                collective_id=0, has_side_effects=True, vmem_limit_bytes=67_043_328),
            name="gossip_sgd",
        )(w_one[0, 0], w_two[0, 0], inputs[0, 0], targets[0, 0])
        return out[0][None, None], out[1][None, None]

    grid_spec = P('row', 'col')
    return jax.shard_map(device_fn, mesh=mesh, in_specs=(grid_spec,) * 4, out_specs=(grid_spec, grid_spec), check_vma=False)
```

time: 1060 us -> 759 us (0.72)
  Pallas kernels: 0 us -> 745 us
  matrix products: 523 us -> 0 us
  waiting for transfers between devices: 386 us -> 0 us
  starting transfers between devices: 64.5 us -> 0 us
  other arithmetic: 49.2 us -> 0 us
  local copies, waits for them, and re-layouts: 29.1 us -> 12.3 us
    pallas_call x0 -> x1, Pallas kernels: none -> 745 us  [device_fn(): pl.pallas_call(functools.partial(kernel, dims), out_shape=(jax.ShapeDtype...]
    dot_general x66 -> x0, matrix products: 523 us -> none  [the longest x9 125 us: local_grads(): jnp.einsum('bd,fd->bf', d_lo, two_lo[layer_idx], preferred_element_type=j...]
    ppermute x72 -> x0, waiting for transfers between devices: 386 us -> none  [the longest x24 210 us: device_fn(): recv_rp = lax.ppermute(wire_vals, 'row', from_row_prev)]
    ppermute x72 -> x0, starting transfers between devices: 64.5 us -> none  [the longest x24 31.9 us: device_fn(): recv_rp = lax.ppermute(wire_vals, 'row', from_row_prev)]
    div x23 -> x0, other arithmetic: 20.5 us -> none  [the longest x14 20.5 us: device_fn(): (own_val + cp_val.astype(jnp.float32) + cn_val.astype(jnp.float32) + rp_v...]
  transfers between devices with their start and end apart: 72 -> 0, of which waited for: 37 -> 0; matrix products, arithmetic and copies ran while one was open for 29% -> 0% of each run, Pallas kernels for 0% -> 0%
where the time goes in v1:
time: 759 us; the launch traced here: 758 us
  Pallas kernels  745 us (98%)
  local copies, waits for them, and re-layouts  12.3 us (2%)
    pallas_call x1, Pallas kernels, device_fn(): pl.pallas_call(functools.partial(kernel, dims), out_shape=(jax.ShapeDtype...  745 us

profile of v1, /device:TPU:0, one launch (start us, length us, event | category | flops | bytes accessed | tf_op | source)
XLA Modules:
  0.0 757.9 jit_solution(182487755646224299)
XLA Ops:
  0.6 744.9 %gossip_sgd.1 = (f32[4,384,1536]{2,1,0:T(8,128)}, f32[4,1536,384]{2,1,0:T(8,128)}, bf16[3,3,12,384,512]{4,3,2,1,0:T(8,128)(2,1)}, bf16[3,3,12,512,384]{4,3,2,1,0:T(8,128)(2,1)}) custom-call(f32[4,384,1536]{2,1,0:T(8,128)} %bitcast.6, f32[4,1536,384]{2,1,0:T(8,128)} %bitcast.7, bf16[3,2048,384]{2,1,0:T(8,128)(2,1)} %bitcast.10, bf16[3,2048,384]{2,1,0:T(8,128)(2,1)} %bitcast.11), custom_call_target="tpu_custom_call" | custom-call | tf_op jit(solution)/shard_map/gossip_sgd/pallas_call | solution.py:263
  745.6 0.0 copy-start
  745.6 8.6 %copy.8 = f32[1,1,4,384,1536]{4,3,2,1,0:T(8,128)} copy(f32[1,1,4,384,1536]{4,3,2,1,0:T(8,128)} %bitcast.9) | data formatting | bytes 18874368
  754.2 0.0 copy-done
  754.2 3.7 copy.9
Async XLA Ops:
  745.6 8.6 %copy-start = (f32[4,1536,384]{2,1,0:T(8,128)S(1)}, f32[4,1536,384]{2,1,0:T(8,128)}, u32[]{:S(2)}) copy-start(f32[4,1536,384]{2,1,0:T(8,128)} %get-tuple-element.5) | copy-start | bytes 28311556

commit v2 on v1

--- a/solution.py
+++ b/solution.py
@@ -38,7 +38,7 @@
 
 
 def kernel(dims, w1_hbm, w2_hbm, x_hbm, tgt_hbm, o1_hbm, o2_hbm, r1_hbm, r2_hbm,
-           m1, m2, l1, l2, hs, err, acc, tgt, act, dpre, nrm, err_lo, nrm_t, err_t, st1, st2,
+           m1, m2, l1, l2, hs, err, acc, tgt, act, dpre, nrm, err_lo, nrm_t, err_t, head_two, st1, st2,
            load_sem, data_sem, stage_sem, out_sem, send_sem, recv_sem):
     n_rows, n_cols, n_steps, n_layers, batch, d_model, d_ff = dims
     f_blk = d_ff // CHUNKS
@@ -64,42 +64,43 @@
         return (pltpu.make_async_copy(x_hbm.at[step], hs.at[0], data_sem.at[0]),
                 pltpu.make_async_copy(tgt_hbm.at[step], tgt, data_sem.at[1]))
 
-    def sends(step, blk):
+    wires = ((m1, l1, r1_hbm, st1), (m2, l2, r2_hbm, st2))
+
+    def sends(step, blk, mat, src=None):
         out = []
         for slot, peer in enumerate(peers):
-            for mat, (src, dst) in enumerate(((l2, r2_hbm), (l1, r1_hbm))):
-                out.append(pltpu.make_async_remote_copy(
-                    src_ref=src.at[blk], dst_ref=dst.at[step, slot, blk],
-                    send_sem=send_sem.at[blk, mat, slot], recv_sem=recv_sem.at[step, blk, mat, slot],
-                    device_id=peer, device_id_type=MESH))
+            out.append(pltpu.make_async_remote_copy(
+                src_ref=wires[mat][1].at[blk] if src is None else src, dst_ref=wires[mat][2].at[step, slot, blk],
+                send_sem=send_sem.at[blk, mat, slot], recv_sem=recv_sem.at[step, blk, mat, slot],
+                device_id=peer, device_id_type=MESH))
         return out
 
-    def start_sends(step, blk):
-        for cp in sends(step, blk):
+    def start_sends(step, blk, mat, src=None):
+        for cp in sends(step, blk, mat, src):
             cp.start()
 
     def sent_early(blk):
         layer, chunk = lax.div(blk, CHUNKS), lax.rem(blk, CHUNKS)
-        head = jnp.logical_and(chunk == 0, layer > 0)
-        return jnp.logical_or(head, blk == n_blk - 2)
+        return jnp.logical_and(chunk < CHUNKS - 1, layer > 0)
 
     def tile_rows(i):
         return pl.ds(pl.multiple_of(i * TILE, TILE), TILE)
 
-    def mix(step, blk):
-        for cp in sends(step, blk):
-            cp.wait_recv()
-        stage = []
-        for slot in range(3):
-            stage.append(pltpu.make_async_copy(r1_hbm.at[step, slot, blk], st1.at[slot], stage_sem.at[0, slot]))
-            stage.append(pltpu.make_async_copy(r2_hbm.at[step, slot, blk], st2.at[slot], stage_sem.at[1, slot]))
+    def mix(step, blk, mats=(0, 1)):
+        for mat in mats:
+            for cp in sends(step, blk, mat):
+                cp.wait_recv()
+        stage = [pltpu.make_async_copy(wires[mat][2].at[step, slot, blk], wires[mat][3].at[slot], stage_sem.at[mat, slot])
+                 for mat in mats for slot in range(3)]
         for cp in stage:
             cp.start()
-        for cp in sends(step, blk):
-            cp.wait_send()
+        for mat in mats:
+            for cp in sends(step, blk, mat):
+                cp.wait_send()
         for cp in stage:
             cp.wait()
-        for own, lo, st in ((m1, l1, st1), (m2, l2, st2)):
+        for mat in mats:
+            own, lo, _, st = wires[mat]
             other = st[2].astype(F32)
             new = (own[blk] + st[0].astype(F32) + st[1].astype(F32) + other + other) * 0.2
             own[blk] = new
@@ -123,6 +124,16 @@
         for cp in data_copies(step):
             cp.wait()
 
+        @pl.when(step > 0)
+        def _():
+            @pl.loop(0, n_blk)
+            def _(k):
+                blk = n_blk - CHUNKS - CHUNKS * lax.div(k, CHUNKS) + lax.rem(k, CHUNKS)
+
+                @pl.when(sent_early(blk))
+                def _():
+                    mix(step - 1, blk)
+
         @pl.loop(0, n_blk)
         def _(blk):
             layer, chunk = lax.div(blk, CHUNKS), lax.rem(blk, CHUNKS)
@@ -133,8 +144,13 @@
                 def _(i):
                     rows = tile_rows(i)
                     hid_f = hs[layer, rows, :].astype(F32)
-                    nrm[rows, :] = (hid_f * inv_rms_of(hid_f)).astype(BF16)
+                    n_f = hid_f * inv_rms_of(hid_f)
+                    nrm[rows, :] = n_f.astype(BF16)
                     acc[rows, :] = hid_f
+
+                    @pl.when(layer == n_layers - 1)
+                    def _():
+                        nrm_t[:, rows] = n_f.T.astype(BF16)
 
             @pl.when(step == 0)
             def _():
@@ -143,16 +159,44 @@
                 l1[blk] = m1[blk].astype(BF16)
                 l2[blk] = m2[blk].astype(BF16)
 
-            @pl.when(step > 0)
+            last_blk = blk == n_blk - 1
+            halves = jnp.logical_and(step > 0, last_blk)
+
+            @pl.when(jnp.logical_and(step > 0, jnp.logical_not(jnp.logical_or(sent_early(blk), last_blk))))
             def _():
                 mix(step - 1, blk)
 
-            @pl.loop(0, n_tiles)
-            def _(i):
-                rows = tile_rows(i)
-                pre = matmul(nrm[rows, :], l1[blk])
-                _, _, half = gelu_half(pre)
-                acc[rows, :] += matmul((pre * half).astype(BF16), l2[blk])
+            @pl.when(jnp.logical_not(halves))
+            def _():
+                @pl.loop(0, n_tiles)
+                def _(i):
+                    rows = tile_rows(i)
+                    pre = matmul(nrm[rows, :], l1[blk])
+                    _, _, half = gelu_half(pre)
+                    a_lo = (pre * half).astype(BF16)
+                    acc[rows, :] += matmul(a_lo, l2[blk])
+
+                    @pl.when(blk == n_blk - CHUNKS)
+                    def _():
+                        act[rows, :] = a_lo
+
+            @pl.when(halves)
+            def _():
+                mix(step - 1, blk, (0,))
+
+                @pl.loop(0, n_tiles)
+                def _(i):
+                    rows = tile_rows(i)
+                    pre = matmul(nrm[rows, :], l1[blk])
+                    _, _, half = gelu_half(pre)
+                    dpre[rows, :] = (pre * half).astype(BF16)
+
+                mix(step - 1, blk, (1,))
+
+                @pl.loop(0, n_tiles)
+                def _(i):
+                    rows = tile_rows(i)
+                    acc[rows, :] += matmul(dpre[rows, :], l2[blk])
 
             @pl.when(jnp.logical_and(chunk == CHUNKS - 1, layer < n_layers - 1))
             def _():
@@ -165,14 +209,24 @@
         def _(i):
             rows = tile_rows(i)
             hid = acc[rows, :].astype(BF16).astype(F32)
-            err[rows, :] = (2.0 / (batch * d_model)) * (hid - tgt[rows, :].astype(F32))
+            e_f = (2.0 / (batch * d_model)) * (hid - tgt[rows, :].astype(F32))
+            err[rows, :] = e_f
+            err_lo[rows, :] = e_f.astype(BF16)
+            err_t[:, rows] = e_f.T.astype(BF16)
+            acc[rows, :] = jnp.zeros((TILE, d_model), F32)
+
+        head_blk = n_blk - CHUNKS
+        upd_head = m2[head_blk] - LEARN_RATE * matmul(err_t[...], act[...]).T
+        m2[head_blk] = upd_head
+        head_two[...] = upd_head.astype(BF16)
+        start_sends(step, head_blk, 1, head_two)
 
         @pl.loop(0, n_blk)
         def _(k):
             layer, chunk = n_layers - 1 - lax.div(k, CHUNKS), lax.rem(k, CHUNKS)
             blk = layer * CHUNKS + chunk
 
-            @pl.when(chunk == 0)
+            @pl.when(jnp.logical_and(chunk == 0, k > 0))
             def _():
                 @pl.loop(0, n_tiles)
                 def _(i):
@@ -197,10 +251,16 @@
                 dpre[rows, :] = d_pre
                 acc[rows, :] += matmul_t(d_pre, l1[blk])
 
-            grad_two = matmul(err_t[...], act[...]).T
-            upd_two = m2[blk] - LEARN_RATE * grad_two
-            m2[blk] = upd_two
-            l2[blk] = upd_two.astype(BF16)
+            @pl.when(k > 0)
+            def _():
+                upd_two = m2[blk] - LEARN_RATE * matmul(err_t[...], act[...]).T
+                m2[blk] = upd_two
+                l2[blk] = upd_two.astype(BF16)
+
+                @pl.when(sent_early(blk))
+                def _():
+                    start_sends(step, blk, 1)
+
             grad_one = matmul(nrm_t[...], dpre[...])
             upd_one = m1[blk] - LEARN_RATE * grad_one
             m1[blk] = upd_one
@@ -208,7 +268,7 @@
 
             @pl.when(sent_early(blk))
             def _():
-                start_sends(step, blk)
+                start_sends(step, blk, 0)
 
             @pl.when(jnp.logical_and(chunk == CHUNKS - 1, layer > 0))
             def _():
@@ -225,7 +285,8 @@
         def _(blk):
             @pl.when(jnp.logical_not(sent_early(blk)))
             def _():
-                start_sends(step, blk)
+                start_sends(step, blk, 0)
+                start_sends(step, blk, 1)
 
         @pl.when(step < n_steps - 1)
         def _():
@@ -285,6 +346,7 @@
                 pltpu.VMEM((batch, d_model), BF16),
                 pltpu.VMEM((d_model, batch), BF16),
                 pltpu.VMEM((d_model, batch), BF16),
+                pltpu.VMEM((f_blk, d_model), BF16),
                 pltpu.VMEM((3, d_model, f_blk), BF16),
                 pltpu.VMEM((3, f_blk, d_model), BF16),
                 pltpu.SemaphoreType.DMA((n_blk, 2)),

time: 759 us -> 698 us (0.920)
  Pallas kernels: 745 us -> 684 us
    pallas_call x1, Pallas kernels: 745 us -> 684 us  [device_fn(): pl.pallas_call(functools.partial(kernel, dims), out_shape=(jax.ShapeDtype...]
where the time goes in v2:
time: 698 us; the launch traced here: 697 us
  Pallas kernels  684 us (98%)
  local copies, waits for them, and re-layouts  12.3 us (2%)
    pallas_call x1, Pallas kernels, device_fn(): pl.pallas_call(functools.partial(kernel, dims), out_shape=(jax.ShapeDtype...  684 us

profile of v2, /device:TPU:0, one launch (start us, length us, event | category | flops | bytes accessed | tf_op | source)
XLA Modules:
  0.0 697.1 jit_solution(2161359402595715053)
XLA Ops:
  0.6 684.1 %gossip_sgd.1 = (f32[4,384,1536]{2,1,0:T(8,128)}, f32[4,1536,384]{2,1,0:T(8,128)}, bf16[3,3,12,384,512]{4,3,2,1,0:T(8,128)(2,1)}, bf16[3,3,12,512,384]{4,3,2,1,0:T(8,128)(2,1)}) custom-call(f32[4,384,1536]{2,1,0:T(8,128)} %bitcast.6, f32[4,1536,384]{2,1,0:T(8,128)} %bitcast.7, bf16[3,2048,384]{2,1,0:T(8,128)(2,1)} %bitcast.10, bf16[3,2048,384]{2,1,0:T(8,128)(2,1)} %bitcast.11), custom_call_target="tpu_custom_call" | custom-call | tf_op jit(solution)/shard_map/gossip_sgd/pallas_call | solution.py:324
  684.7 0.0 copy-start
  684.8 8.6 %copy.8 = f32[1,1,4,384,1536]{4,3,2,1,0:T(8,128)} copy(f32[1,1,4,384,1536]{4,3,2,1,0:T(8,128)} %bitcast.9) | data formatting | bytes 18874368
  693.4 0.0 copy-done
  693.4 3.7 copy.9
Async XLA Ops:
  684.7 8.6 %copy-start = (f32[4,1536,384]{2,1,0:T(8,128)S(1)}, f32[4,1536,384]{2,1,0:T(8,128)}, u32[]{:S(2)}) copy-start(f32[4,1536,384]{2,1,0:T(8,128)} %get-tuple-element.5) | copy-start | bytes 28311556

commit v3 on v2

--- a/solution.py
+++ b/solution.py
@@ -17,6 +17,7 @@
 BF16 = jnp.bfloat16
 CHUNKS = 3
 TILE = 512
+SUB = 256
 
 
 def matmul(lhs, rhs):
@@ -38,12 +39,14 @@
 
 
 def kernel(dims, w1_hbm, w2_hbm, x_hbm, tgt_hbm, o1_hbm, o2_hbm, r1_hbm, r2_hbm,
-           m1, m2, l1, l2, hs, err, acc, tgt, act, dpre, nrm, err_lo, nrm_t, err_t, head_two, st1, st2,
+           m1, m2, l1, l2, hs, err, acc, tgt, ff, nrm, err_lo, nrm_t, err_t, head_two, st1, st2,
            load_sem, data_sem, stage_sem, out_sem, send_sem, recv_sem):
     n_rows, n_cols, n_steps, n_layers, batch, d_model, d_ff = dims
     f_blk = d_ff // CHUNKS
     n_blk = n_layers * CHUNKS
     n_tiles = batch // TILE
+    act, dpre = ff.at[0], ff.at[1]
+    pieces = [slice(i, i + SUB) for i in range(0, batch, SUB)]
     row, col = lax.axis_index("row"), lax.axis_index("col")
     peers = ((row, lax.rem(col + 1, n_cols)), (row, lax.rem(col + n_cols - 1, n_cols)), (n_rows - 1 - row, col))
 
@@ -60,9 +63,11 @@
         return (pltpu.make_async_copy(m1.at[blk], o1_hbm.at[layer, :, cols_of(blk)], out_sem.at[blk, 0]),
                 pltpu.make_async_copy(m2.at[blk], o2_hbm.at[layer, cols_of(blk), :], out_sem.at[blk, 1]))
 
-    def data_copies(step):
-        return (pltpu.make_async_copy(x_hbm.at[step], hs.at[0], data_sem.at[0]),
-                pltpu.make_async_copy(tgt_hbm.at[step], tgt, data_sem.at[1]))
+    def input_copy(step):
+        return pltpu.make_async_copy(x_hbm.at[step], hs.at[0], data_sem.at[0])
+
+    def target_copy(step):
+        return pltpu.make_async_copy(tgt_hbm.at[step], tgt, data_sem.at[1])
 
     wires = ((m1, l1, r1_hbm, st1), (m2, l2, r2_hbm, st2))
 
@@ -109,20 +114,57 @@
     barrier = pltpu.get_barrier_semaphore()
     for peer in peers:
         pl.semaphore_signal(barrier, inc=1, device_id=peer, device_id_type=MESH)
-    for cp in data_copies(0):
-        cp.start()
-
-    @pl.loop(0, n_blk)
-    def _(blk):
+    input_copy(0).start()
+
+    for blk in range(CHUNKS):
         for cp in load_copies(blk):
             cp.start()
-
-    pl.semaphore_wait(barrier, 3)
+    target_copy(0).start()
+
+    def first_forward():
+        @pl.loop(0, n_layers)
+        def _(layer):
+            base = layer * CHUNKS
+
+            @pl.when(layer < n_layers - 1)
+            def _():
+                for c in range(CHUNKS):
+                    for cp in load_copies(lax.min(base + CHUNKS + c, n_blk - 1)):
+                        cp.start()
+
+            for c in range(CHUNKS):
+                for cp in load_copies(base + c):
+                    cp.wait()
+                l1[base + c] = m1[base + c].astype(BF16)
+                l2[base + c] = m2[base + c].astype(BF16)
+
+            behind = None
+            for rows in pieces + [None]:
+                pre = []
+                if rows is not None:
+                    hid_f = hs[layer, rows, :].astype(F32)
+                    n_lo = (hid_f * inv_rms_of(hid_f)).astype(BF16)
+                    nrm[rows, :] = n_lo
+                    pre = [matmul(n_lo, l1[base + c]) for c in range(CHUNKS)]
+                if behind is not None:
+                    b_rows, b_hid, b_act = behind
+                    mlp = matmul(b_act[0], l2[base])
+                    for c in range(1, CHUNKS):
+                        mlp += matmul(b_act[c], l2[base + c])
+                    hs[layer + 1, b_rows, :] = (b_hid + mlp).astype(BF16)
+                if rows is not None:
+                    b_act = [(z * gelu_half(z)[2]).astype(BF16) for z in pre]
+                    act[rows, :] = b_act[0]
+                    behind = (rows, hid_f, b_act)
+
 
     @pl.loop(0, n_steps)
     def _(step):
-        for cp in data_copies(step):
-            cp.wait()
+        input_copy(step).wait()
+
+        @pl.when(step == 0)
+        def _():
+            first_forward()
 
         @pl.when(step > 0)
         def _():
@@ -134,9 +176,10 @@
                 def _():
                     mix(step - 1, blk)
 
-        @pl.loop(0, n_blk)
+        @pl.loop(0, lax.select(step > 0, n_blk, 0))
         def _(blk):
             layer, chunk = lax.div(blk, CHUNKS), lax.rem(blk, CHUNKS)
+            last_blk = blk == n_blk - 1
 
             @pl.when(chunk == 0)
             def _():
@@ -148,67 +191,47 @@
                     nrm[rows, :] = n_f.astype(BF16)
                     acc[rows, :] = hid_f
 
-                    @pl.when(layer == n_layers - 1)
-                    def _():
-                        nrm_t[:, rows] = n_f.T.astype(BF16)
-
-            @pl.when(step == 0)
-            def _():
-                for cp in load_copies(blk):
-                    cp.wait()
-                l1[blk] = m1[blk].astype(BF16)
-                l2[blk] = m2[blk].astype(BF16)
-
-            last_blk = blk == n_blk - 1
-            halves = jnp.logical_and(step > 0, last_blk)
-
-            @pl.when(jnp.logical_and(step > 0, jnp.logical_not(jnp.logical_or(sent_early(blk), last_blk))))
+            @pl.when(jnp.logical_not(jnp.logical_or(sent_early(blk), last_blk)))
             def _():
                 mix(step - 1, blk)
 
-            @pl.when(jnp.logical_not(halves))
+            @pl.when(jnp.logical_not(last_blk))
+            def _():
+                keep = lax.select(blk == n_blk - CHUNKS, 0, 1)
+                behind = None
+                for rows in pieces + [None]:
+                    if rows is not None:
+                        pre = matmul(nrm[rows, :], l1[blk])
+                    if behind is not None:
+                        acc[behind[0], :] += matmul(behind[1], l2[blk])
+                    if rows is not None:
+                        a_lo = (pre * gelu_half(pre)[2]).astype(BF16)
+                        ff[keep, rows, :] = a_lo
+                        behind = (rows, a_lo)
+
+            @pl.when(last_blk)
+            def _():
+                mix(step - 1, blk, (0,))
+                for rows in pieces:
+                    pre = matmul(nrm[rows, :], l1[blk])
+                    dpre[rows, :] = (pre * gelu_half(pre)[2]).astype(BF16)
+                mix(step - 1, blk, (1,))
+                for rows in pieces:
+                    hs[n_layers, rows, :] = (acc[rows, :] + matmul(dpre[rows, :], l2[blk])).astype(BF16)
+
+            @pl.when(jnp.logical_and(chunk == CHUNKS - 1, layer < n_layers - 1))
             def _():
                 @pl.loop(0, n_tiles)
                 def _(i):
                     rows = tile_rows(i)
-                    pre = matmul(nrm[rows, :], l1[blk])
-                    _, _, half = gelu_half(pre)
-                    a_lo = (pre * half).astype(BF16)
-                    acc[rows, :] += matmul(a_lo, l2[blk])
-
-                    @pl.when(blk == n_blk - CHUNKS)
-                    def _():
-                        act[rows, :] = a_lo
-
-            @pl.when(halves)
-            def _():
-                mix(step - 1, blk, (0,))
-
-                @pl.loop(0, n_tiles)
-                def _(i):
-                    rows = tile_rows(i)
-                    pre = matmul(nrm[rows, :], l1[blk])
-                    _, _, half = gelu_half(pre)
-                    dpre[rows, :] = (pre * half).astype(BF16)
-
-                mix(step - 1, blk, (1,))
-
-                @pl.loop(0, n_tiles)
-                def _(i):
-                    rows = tile_rows(i)
-                    acc[rows, :] += matmul(dpre[rows, :], l2[blk])
-
-            @pl.when(jnp.logical_and(chunk == CHUNKS - 1, layer < n_layers - 1))
-            def _():
-                @pl.loop(0, n_tiles)
-                def _(i):
-                    rows = tile_rows(i)
-                    hs[lax.min(layer + 1, n_layers - 1), rows, :] = acc[rows, :].astype(BF16)
+                    hs[layer + 1, rows, :] = acc[rows, :].astype(BF16)
+
+        target_copy(step).wait()
 
         @pl.loop(0, n_tiles)
         def _(i):
             rows = tile_rows(i)
-            hid = acc[rows, :].astype(BF16).astype(F32)
+            hid = hs[n_layers, rows, :].astype(F32)
             e_f = (2.0 / (batch * d_model)) * (hid - tgt[rows, :].astype(F32))
             err[rows, :] = e_f
             err_lo[rows, :] = e_f.astype(BF16)
@@ -219,7 +242,17 @@
         upd_head = m2[head_blk] - LEARN_RATE * matmul(err_t[...], act[...]).T
         m2[head_blk] = upd_head
         head_two[...] = upd_head.astype(BF16)
+
+        @pl.when(step == 0)
+        def _():
+            pl.semaphore_wait(barrier, 3)
+
         start_sends(step, head_blk, 1, head_two)
+
+        @pl.loop(0, n_tiles)
+        def _(i):
+            rows = tile_rows(i)
+            nrm_t[:, rows] = nrm[rows, :].astype(F32).T.astype(BF16)
 
         @pl.loop(0, n_blk)
         def _(k):
@@ -290,8 +323,8 @@
 
         @pl.when(step < n_steps - 1)
         def _():
-            for cp in data_copies(lax.min(step + 1, n_steps - 1)):
-                cp.start()
+            input_copy(lax.min(step + 1, n_steps - 1)).start()
+            target_copy(lax.min(step + 1, n_steps - 1)).start()
 
     for early in (True, False):
         @pl.loop(0, n_blk)
@@ -336,12 +369,11 @@
                 pltpu.VMEM((n_blk, f_blk, d_model), F32),
                 pltpu.VMEM((n_blk, d_model, f_blk), BF16),
                 pltpu.VMEM((n_blk, f_blk, d_model), BF16),
-                pltpu.VMEM((n_layers, batch, d_model), BF16),
+                pltpu.VMEM((n_layers + 1, batch, d_model), BF16),
                 pltpu.VMEM((batch, d_model), F32),
                 pltpu.VMEM((batch, d_model), F32),
                 pltpu.VMEM((batch, d_model), BF16),
-                pltpu.VMEM((batch, f_blk), BF16),
-                pltpu.VMEM((batch, f_blk), BF16),
+                pltpu.VMEM((2, batch, f_blk), BF16),
                 pltpu.VMEM((batch, d_model), BF16),
                 pltpu.VMEM((batch, d_model), BF16),
                 pltpu.VMEM((d_model, batch), BF16),

time: 698 us -> 679 us (0.973)
  Pallas kernels: 684 us -> 665 us
    pallas_call x1, Pallas kernels: 684 us -> 665 us  [device_fn(): pl.pallas_call(functools.partial(kernel, dims), out_shape=(jax.ShapeDtype...]
where the time goes in v3:
time: 679 us; the launch traced here: 678 us
  Pallas kernels  665 us (98%)
  local copies, waits for them, and re-layouts  12.4 us (2%)
    pallas_call x1, Pallas kernels, device_fn(): pl.pallas_call(functools.partial(kernel, dims), out_shape=(jax.ShapeDtype...  665 us

profile of v3, /device:TPU:0, one launch (start us, length us, event | category | flops | bytes accessed | tf_op | source)
XLA Modules:
  0.0 678.0 jit_solution(9330510263368724820)
XLA Ops:
  0.6 665.0 %gossip_sgd.1 = (f32[4,384,1536]{2,1,0:T(8,128)}, f32[4,1536,384]{2,1,0:T(8,128)}, bf16[3,3,12,384,512]{4,3,2,1,0:T(8,128)(2,1)}, bf16[3,3,12,512,384]{4,3,2,1,0:T(8,128)(2,1)}) custom-call(f32[4,384,1536]{2,1,0:T(8,128)} %bitcast.6, f32[4,1536,384]{2,1,0:T(8,128)} %bitcast.7, bf16[3,2048,384]{2,1,0:T(8,128)(2,1)} %bitcast.10, bf16[3,2048,384]{2,1,0:T(8,128)(2,1)} %bitcast.11), custom_call_target="tpu_custom_call" | custom-call | tf_op jit(solution)/shard_map/gossip_sgd/pallas_call | solution.py:357
  665.6 0.0 copy-start
  665.7 8.6 %copy.8 = f32[1,1,4,384,1536]{4,3,2,1,0:T(8,128)} copy(f32[1,1,4,384,1536]{4,3,2,1,0:T(8,128)} %bitcast.9) | data formatting | bytes 18874368
  674.3 0.0 copy-done
  674.3 3.7 copy.9
Async XLA Ops:
  665.6 8.6 %copy-start = (f32[4,1536,384]{2,1,0:T(8,128)S(1)}, f32[4,1536,384]{2,1,0:T(8,128)}, u32[]{:S(2)}) copy-start(f32[4,1536,384]{2,1,0:T(8,128)} %get-tuple-element.5) | copy-start | bytes 28311556

commit v4 on v3

--- a/solution.py
+++ b/solution.py
@@ -58,10 +58,11 @@
         return (pltpu.make_async_copy(w1_hbm.at[layer, :, cols_of(blk)], m1.at[blk], load_sem.at[blk, 0]),
                 pltpu.make_async_copy(w2_hbm.at[layer, cols_of(blk), :], m2.at[blk], load_sem.at[blk, 1]))
 
-    def out_copies(blk):
+    def out_copy(blk, mat):
         layer = lax.div(blk, CHUNKS)
-        return (pltpu.make_async_copy(m1.at[blk], o1_hbm.at[layer, :, cols_of(blk)], out_sem.at[blk, 0]),
-                pltpu.make_async_copy(m2.at[blk], o2_hbm.at[layer, cols_of(blk), :], out_sem.at[blk, 1]))
+        if mat == 0:
+            return pltpu.make_async_copy(m1.at[blk], o1_hbm.at[layer, :, cols_of(blk)], out_sem.at[blk, 0])
+        return pltpu.make_async_copy(m2.at[blk], o2_hbm.at[layer, cols_of(blk), :], out_sem.at[blk, 1])
 
     def input_copy(step):
         return pltpu.make_async_copy(x_hbm.at[step], hs.at[0], data_sem.at[0])
@@ -247,7 +248,11 @@
         def _():
             pl.semaphore_wait(barrier, 3)
 
-        start_sends(step, head_blk, 1, head_two)
+        at_once = jnp.logical_or(step > 0, lax.rem(row + col, 2) == 0)
+
+        @pl.when(at_once)
+        def _():
+            start_sends(step, head_blk, 1, head_two)
 
         @pl.loop(0, n_tiles)
         def _(i):
@@ -299,6 +304,10 @@
             m1[blk] = upd_one
             l1[blk] = upd_one.astype(BF16)
 
+            @pl.when(jnp.logical_and(k == 0, jnp.logical_not(at_once)))
+            def _():
+                start_sends(step, head_blk, 1, head_two)
+
             @pl.when(sent_early(blk))
             def _():
                 start_sends(step, blk, 0)
@@ -333,14 +342,14 @@
 
             @pl.when(turn)
             def _():
-                mix(n_steps - 1, blk)
-                for cp in out_copies(blk):
-                    cp.start()
+                for mat in range(2):
+                    mix(n_steps - 1, blk, (mat,))
+                    out_copy(blk, mat).start()
 
     @pl.loop(0, n_blk)
     def _(blk):
-        for cp in out_copies(blk):
-            cp.wait()
+        for mat in range(2):
+            out_copy(blk, mat).wait()
 
 
 def solution(mesh):

time: 679 us -> 679 us (level)
  no operation moved by 1% of the time
where the time goes in v4:
time: 679 us; the launch traced here: 678 us
  Pallas kernels  665 us (98%)
  local copies, waits for them, and re-layouts  12.3 us (2%)
    pallas_call x1, Pallas kernels, device_fn(): pl.pallas_call(functools.partial(kernel, dims), out_shape=(jax.ShapeDtype...  665 us

profile of v4, /device:TPU:0, one launch (start us, length us, event | category | flops | bytes accessed | tf_op | source)
XLA Modules:
  0.0 677.9 jit_solution(5807493568694602606)
XLA Ops:
  0.6 664.9 %gossip_sgd.1 = (f32[4,384,1536]{2,1,0:T(8,128)}, f32[4,1536,384]{2,1,0:T(8,128)}, bf16[3,3,12,384,512]{4,3,2,1,0:T(8,128)(2,1)}, bf16[3,3,12,512,384]{4,3,2,1,0:T(8,128)(2,1)}) custom-call(f32[4,384,1536]{2,1,0:T(8,128)} %bitcast.6, f32[4,1536,384]{2,1,0:T(8,128)} %bitcast.7, bf16[3,2048,384]{2,1,0:T(8,128)(2,1)} %bitcast.10, bf16[3,2048,384]{2,1,0:T(8,128)(2,1)} %bitcast.11), custom_call_target="tpu_custom_call" | custom-call | tf_op jit(solution)/shard_map/gossip_sgd/pallas_call | solution.py:366
  665.5 0.0 copy-start
  665.5 8.6 %copy.8 = f32[1,1,4,384,1536]{4,3,2,1,0:T(8,128)} copy(f32[1,1,4,384,1536]{4,3,2,1,0:T(8,128)} %bitcast.9) | data formatting | bytes 18874368
  674.1 0.0 copy-done
  674.1 3.7 copy.9
Async XLA Ops:
  665.5 8.6 %copy-start = (f32[4,1536,384]{2,1,0:T(8,128)S(1)}, f32[4,1536,384]{2,1,0:T(8,128)}, u32[]{:S(2)}) copy-start(f32[4,1536,384]{2,1,0:T(8,128)} %get-tuple-element.5) | copy-start | bytes 28311556

commit v5 on v4

--- a/solution.py
+++ b/solution.py
@@ -17,6 +17,7 @@
 BF16 = jnp.bfloat16
 CHUNKS = 3
 TILE = 512
+VMEM_BYTES = 47_000_000
 SUB = 256
 
 
@@ -38,9 +39,9 @@
     return lax.rsqrt(jnp.mean(hid_f * hid_f, axis=-1, keepdims=True) + NORM_EPS)
 
 
-def kernel(dims, w1_hbm, w2_hbm, x_hbm, tgt_hbm, o1_hbm, o2_hbm, r1_hbm, r2_hbm,
-           m1, m2, l1, l2, hs, err, acc, tgt, ff, nrm, err_lo, nrm_t, err_t, head_two, st1, st2,
-           load_sem, data_sem, stage_sem, out_sem, send_sem, recv_sem):
+def kernel(dims, w1_hbm, w2_hbm, x_hbm, tgt_hbm, m1, m2, r1_hbm, r2_hbm,
+           l1, l2, hs, err, acc, tgt, ff, nrm, err_lo, nrm_t, err_t, head_two, st1, st2,
+           load_sem, data_sem, stage_sem, send_sem, recv_sem):
     n_rows, n_cols, n_steps, n_layers, batch, d_model, d_ff = dims
     f_blk = d_ff // CHUNKS
     n_blk = n_layers * CHUNKS
@@ -55,14 +56,8 @@
 
     def load_copies(blk):
         layer = lax.div(blk, CHUNKS)
-        return (pltpu.make_async_copy(w1_hbm.at[layer, :, cols_of(blk)], m1.at[blk], load_sem.at[blk, 0]),
+        return (pltpu.make_async_copy(w1_hbm.at[layer, :, cols_of(blk)], m1.at[layer, :, cols_of(blk)], load_sem.at[blk, 0]),
                 pltpu.make_async_copy(w2_hbm.at[layer, cols_of(blk), :], m2.at[blk], load_sem.at[blk, 1]))
-
-    def out_copy(blk, mat):
-        layer = lax.div(blk, CHUNKS)
-        if mat == 0:
-            return pltpu.make_async_copy(m1.at[blk], o1_hbm.at[layer, :, cols_of(blk)], out_sem.at[blk, 0])
-        return pltpu.make_async_copy(m2.at[blk], o2_hbm.at[layer, cols_of(blk), :], out_sem.at[blk, 1])
 
     def input_copy(step):
         return pltpu.make_async_copy(x_hbm.at[step], hs.at[0], data_sem.at[0])
@@ -70,7 +65,7 @@
     def target_copy(step):
         return pltpu.make_async_copy(tgt_hbm.at[step], tgt, data_sem.at[1])
 
-    wires = ((m1, l1, r1_hbm, st1), (m2, l2, r2_hbm, st2))
+    wires = ((None, l1, r1_hbm, st1), (None, l2, r2_hbm, st2))
 
     def sends(step, blk, mat, src=None):
         out = []
@@ -106,10 +101,11 @@
         for cp in stage:
             cp.wait()
         for mat in mats:
-            own, lo, _, st = wires[mat]
+            _, lo, _, st = wires[mat]
+            own, at = (m1, (lax.div(blk, CHUNKS), slice(None), cols_of(blk))) if mat == 0 else (m2, (blk,))
             other = st[2].astype(F32)
-            new = (own[blk] + st[0].astype(F32) + st[1].astype(F32) + other + other) * 0.2
-            own[blk] = new
+            new = (own[at] + st[0].astype(F32) + st[1].astype(F32) + other + other) * 0.2
+            own[at] = new
             lo[blk] = new.astype(BF16)
 
     barrier = pltpu.get_barrier_semaphore()
@@ -136,7 +132,7 @@
             for c in range(CHUNKS):
                 for cp in load_copies(base + c):
                     cp.wait()
-                l1[base + c] = m1[base + c].astype(BF16)
+                l1[base + c] = m1[layer, :, c * f_blk:(c + 1) * f_blk].astype(BF16)
                 l2[base + c] = m2[base + c].astype(BF16)
 
             behind = None
@@ -300,8 +296,8 @@
                     start_sends(step, blk, 1)
 
             grad_one = matmul(nrm_t[...], dpre[...])
-            upd_one = m1[blk] - LEARN_RATE * grad_one
-            m1[blk] = upd_one
+            upd_one = m1[layer, :, cols_of(blk)] - LEARN_RATE * grad_one
+            m1[layer, :, cols_of(blk)] = upd_one
             l1[blk] = upd_one.astype(BF16)
 
             @pl.when(jnp.logical_and(k == 0, jnp.logical_not(at_once)))
@@ -344,12 +340,6 @@
             def _():
                 for mat in range(2):
                     mix(n_steps - 1, blk, (mat,))
-                    out_copy(blk, mat).start()
-
-    @pl.loop(0, n_blk)
-    def _(blk):
-        for mat in range(2):
-            out_copy(blk, mat).wait()
 
 
 def solution(mesh):
@@ -363,19 +353,18 @@
         n_blk = n_layers * CHUNKS
         dims = (n_rows, n_cols, n_steps, n_layers, batch, d_model, d_ff)
         any_spec = pl.BlockSpec(memory_space=pl.ANY)
+        vmem_spec = pl.BlockSpec(memory_space=pltpu.VMEM)
         out = pl.pallas_call(
             functools.partial(kernel, dims),
             out_shape=(
-                jax.ShapeDtypeStruct((n_layers, d_model, d_ff), F32),
-                jax.ShapeDtypeStruct((n_layers, d_ff, d_model), F32),
+                pltpu.VMEM((n_layers, d_model, d_ff), F32),
+                pltpu.VMEM((n_blk, f_blk, d_model), F32),
                 jax.ShapeDtypeStruct((n_steps, 3, n_blk, d_model, f_blk), BF16),
                 jax.ShapeDtypeStruct((n_steps, 3, n_blk, f_blk, d_model), BF16),
             ),
             in_specs=[any_spec] * 4,
-            out_specs=(any_spec,) * 4,
+            out_specs=(vmem_spec, vmem_spec, any_spec, any_spec),
             scratch_shapes=[
-                pltpu.VMEM((n_blk, d_model, f_blk), F32),
-                pltpu.VMEM((n_blk, f_blk, d_model), F32),
                 pltpu.VMEM((n_blk, d_model, f_blk), BF16),
                 pltpu.VMEM((n_blk, f_blk, d_model), BF16),
                 pltpu.VMEM((n_layers + 1, batch, d_model), BF16),
@@ -393,15 +382,14 @@
                 pltpu.SemaphoreType.DMA((n_blk, 2)),
                 pltpu.SemaphoreType.DMA((2,)),
                 pltpu.SemaphoreType.DMA((2, 3)),
-                pltpu.SemaphoreType.DMA((n_blk, 2)),
                 pltpu.SemaphoreType.DMA((n_blk, 2, 3)),
                 pltpu.SemaphoreType.DMA((n_steps, n_blk, 2, 3)),
             ],
             compiler_params=pltpu.CompilerParams(
-                collective_id=0, has_side_effects=True, vmem_limit_bytes=67_043_328),
+                collective_id=0, has_side_effects=True, vmem_limit_bytes=VMEM_BYTES),
             name="gossip_sgd",
         )(w_one[0, 0], w_two[0, 0], inputs[0, 0], targets[0, 0])
-        return out[0][None, None], out[1][None, None]
+        return out[0][None, None], out[1].reshape(w_two.shape)
 
     grid_spec = P('row', 'col')
     return jax.shard_map(device_fn, mesh=mesh, in_specs=(grid_spec,) * 4, out_specs=(grid_spec, grid_spec), check_vma=False)

time: 679 us -> 673 us (level)
  no operation moved by 1% of the time
where the time goes in v5:
time: 673 us; the launch traced here: 672 us
  Pallas kernels  664 us (99%)
  local copies, waits for them, and re-layouts  7.49 us (1%)
    pallas_call x1, Pallas kernels, device_fn(): pl.pallas_call(functools.partial(kernel, dims), out_shape=(pltpu.VMEM((n_...  664 us

profile of v5, /device:TPU:0, one launch (start us, length us, event | category | flops | bytes accessed | tf_op | source)
XLA Modules:
  0.0 672.2 jit_solution(14024321890095484796)
XLA Ops:
  0.6 664.0 %gossip_sgd.1 = (f32[4,384,1536]{2,1,0:T(8,128)S(1)}, f32[12,512,384]{2,1,0:T(8,128)S(1)}, bf16[3,3,12,384,512]{4,3,2,1,0:T(8,128)(2,1)}, bf16[3,3,12,512,384]{4,3,2,1,0:T(8,128)(2,1)}) custom-call(f32[4,384,1536]{2,1,0:T(8,128)} %bitcast.8, f32[4,1536,384]{2,1,0:T(8,128)} %bitcast.9, bf16[3,2048,384]{2,1,0:T(8,128)(2,1)} %bitcast.10, ...), custom_call_target="tpu_custom_call" | custom-call | tf_op jit(solution)/shard_map/gossip_sgd/pallas_call | solution.py:357
  664.7 3.7 copy.8
  668.4 3.7 copy.9

commit v6 on v5

--- a/solution.py
+++ b/solution.py
@@ -40,7 +40,7 @@
 
 
 def kernel(dims, w1_hbm, w2_hbm, x_hbm, tgt_hbm, m1, m2, r1_hbm, r2_hbm,
-           l1, l2, hs, err, acc, tgt, ff, nrm, err_lo, nrm_t, err_t, head_two, st1, st2,
+           l1, l2, hs, err, acc, tgt, ff, nrm, err_lo, nrm_t, err_t, head_two, tail_one, tail_two, st1, st2,
            load_sem, data_sem, stage_sem, send_sem, recv_sem):
     n_rows, n_cols, n_steps, n_layers, batch, d_model, d_ff = dims
     f_blk = d_ff // CHUNKS
@@ -84,6 +84,17 @@
         layer, chunk = lax.div(blk, CHUNKS), lax.rem(blk, CHUNKS)
         return jnp.logical_and(chunk < CHUNKS - 1, layer > 0)
 
+    def is_tail(blk):
+        return jnp.logical_and(lax.rem(blk, CHUNKS) == CHUNKS - 1, blk >= CHUNKS)
+
+    def tail_src(blk, mat):
+        return (tail_one, tail_two)[mat].at[lax.max(lax.div(blk, CHUNKS) - 1, 0)]
+
+    def wait_sent(step, blk, mats=(0, 1)):
+        for mat in mats:
+            for cp in sends(step, blk, mat):
+                cp.wait_send()
+
     def tile_rows(i):
         return pl.ds(pl.multiple_of(i * TILE, TILE), TILE)
 
@@ -95,9 +106,11 @@
                  for mat in mats for slot in range(3)]
         for cp in stage:
             cp.start()
-        for mat in mats:
-            for cp in sends(step, blk, mat):
-                cp.wait_send()
+
+        @pl.when(jnp.logical_not(is_tail(blk)))
+        def _():
+            wait_sent(step, blk, mats)
+
         for cp in stage:
             cp.wait()
         for mat in mats:
@@ -291,6 +304,11 @@
                 m2[blk] = upd_two
                 l2[blk] = upd_two.astype(BF16)
 
+                @pl.when(jnp.logical_and(k == 1, jnp.logical_not(at_once)))
+                def _():
+                    start_sends(step, head_blk, 1, head_two)
+                    start_sends(step, head_blk, 0)
+
                 @pl.when(sent_early(blk))
                 def _():
                     start_sends(step, blk, 1)
@@ -300,13 +318,18 @@
             m1[layer, :, cols_of(blk)] = upd_one
             l1[blk] = upd_one.astype(BF16)
 
-            @pl.when(jnp.logical_and(k == 0, jnp.logical_not(at_once)))
-            def _():
-                start_sends(step, head_blk, 1, head_two)
-
-            @pl.when(sent_early(blk))
+            @pl.when(jnp.logical_and(sent_early(blk), jnp.logical_or(k > 0, at_once)))
             def _():
                 start_sends(step, blk, 0)
+
+            @pl.when(is_tail(blk))
+            def _():
+                @pl.when(step > 0)
+                def _():
+                    wait_sent(step - 1, blk)
+
+                tail_src(blk, 0)[...] = l1[blk]
+                tail_src(blk, 1)[...] = l2[blk]
 
             @pl.when(jnp.logical_and(chunk == CHUNKS - 1, layer > 0))
             def _():
@@ -321,10 +344,15 @@
 
         @pl.loop(0, n_blk)
         def _(blk):
-            @pl.when(jnp.logical_not(sent_early(blk)))
-            def _():
-                start_sends(step, blk, 0)
-                start_sends(step, blk, 1)
+            @pl.when(is_tail(blk))
+            def _():
+                for mat in range(2):
+                    start_sends(step, blk, mat, tail_src(blk, mat))
+
+            @pl.when(jnp.logical_not(jnp.logical_or(sent_early(blk), is_tail(blk))))
+            def _():
+                for mat in range(2):
+                    start_sends(step, blk, mat)
 
         @pl.when(step < n_steps - 1)
         def _():
@@ -340,6 +368,12 @@
             def _():
                 for mat in range(2):
                     mix(n_steps - 1, blk, (mat,))
+
+    @pl.loop(0, n_blk)
+    def _(blk):
+        @pl.when(is_tail(blk))
+        def _():
+            wait_sent(n_steps - 1, blk)
 
 
 def solution(mesh):
@@ -377,6 +411,8 @@
                 pltpu.VMEM((d_model, batch), BF16),
                 pltpu.VMEM((d_model, batch), BF16),
                 pltpu.VMEM((f_blk, d_model), BF16),
+                pltpu.VMEM((n_layers - 1, d_model, f_blk), BF16),
+                pltpu.VMEM((n_layers - 1, f_blk, d_model), BF16),
                 pltpu.VMEM((3, d_model, f_blk), BF16),
                 pltpu.VMEM((3, f_blk, d_model), BF16),
                 pltpu.SemaphoreType.DMA((n_blk, 2)),

time: 673 us -> 670 us (level)
  no operation moved by 1% of the time
where the time goes in v6:
time: 670 us; the launch traced here: 669 us
  Pallas kernels  660 us (99%)
  local copies, waits for them, and re-layouts  7.49 us (1%)
    pallas_call x1, Pallas kernels, device_fn(): pl.pallas_call(functools.partial(kernel, dims), out_shape=(pltpu.VMEM((n_...  660 us

profile of v6, /device:TPU:0, one launch (start us, length us, event | category | flops | bytes accessed | tf_op | source)
XLA Modules:
  0.0 668.5 jit_solution(510397436054933472)
XLA Ops:
  0.6 660.4 %gossip_sgd.1 = (f32[4,384,1536]{2,1,0:T(8,128)S(1)}, f32[12,512,384]{2,1,0:T(8,128)S(1)}, bf16[3,3,12,384,512]{4,3,2,1,0:T(8,128)(2,1)}, bf16[3,3,12,512,384]{4,3,2,1,0:T(8,128)(2,1)}) custom-call(f32[4,384,1536]{2,1,0:T(8,128)} %bitcast.8, f32[4,1536,384]{2,1,0:T(8,128)} %bitcast.9, bf16[3,2048,384]{2,1,0:T(8,128)(2,1)} %bitcast.10, ...), custom_call_target="tpu_custom_call" | custom-call | tf_op jit(solution)/shard_map/gossip_sgd/pallas_call | solution.py:391
  661.1 3.7 copy.8
  664.8 3.7 copy.9

commit v7 on v6

--- a/solution.py
+++ b/solution.py
@@ -130,6 +130,13 @@
         for cp in load_copies(blk):
             cp.start()
     target_copy(0).start()
+
+    def loss_grad(rows, hid, size):
+        e_f = (2.0 / (batch * d_model)) * (hid.astype(F32) - tgt[rows, :].astype(F32))
+        err[rows, :] = e_f
+        err_lo[rows, :] = e_f.astype(BF16)
+        err_t[:, rows] = e_f.T.astype(BF16)
+        acc[rows, :] = jnp.zeros((size, d_model), F32)
 
     def first_forward():
         @pl.loop(0, n_layers)
@@ -225,9 +232,10 @@
                 for rows in pieces:
                     pre = matmul(nrm[rows, :], l1[blk])
                     dpre[rows, :] = (pre * gelu_half(pre)[2]).astype(BF16)
+                target_copy(step).wait()
                 mix(step - 1, blk, (1,))
                 for rows in pieces:
-                    hs[n_layers, rows, :] = (acc[rows, :] + matmul(dpre[rows, :], l2[blk])).astype(BF16)
+                    loss_grad(rows, (acc[rows, :] + matmul(dpre[rows, :], l2[blk])).astype(BF16), SUB)
 
             @pl.when(jnp.logical_and(chunk == CHUNKS - 1, layer < n_layers - 1))
             def _():
@@ -236,17 +244,14 @@
                     rows = tile_rows(i)
                     hs[layer + 1, rows, :] = acc[rows, :].astype(BF16)
 
-        target_copy(step).wait()
-
-        @pl.loop(0, n_tiles)
-        def _(i):
-            rows = tile_rows(i)
-            hid = hs[n_layers, rows, :].astype(F32)
-            e_f = (2.0 / (batch * d_model)) * (hid - tgt[rows, :].astype(F32))
-            err[rows, :] = e_f
-            err_lo[rows, :] = e_f.astype(BF16)
-            err_t[:, rows] = e_f.T.astype(BF16)
-            acc[rows, :] = jnp.zeros((TILE, d_model), F32)
+        @pl.when(step == 0)
+        def _():
+            target_copy(0).wait()
+
+            @pl.loop(0, n_tiles)
+            def _(i):
+                rows = tile_rows(i)
+                loss_grad(rows, hs[n_layers, rows, :], TILE)
 
         head_blk = n_blk - CHUNKS
         upd_head = m2[head_blk] - LEARN_RATE * matmul(err_t[...], act[...]).T
@@ -287,16 +292,20 @@
                     err_t[:, rows] = e_f.T.astype(BF16)
                     acc[rows, :] = jnp.zeros((TILE, d_model), F32)
 
-            @pl.loop(0, n_tiles)
-            def _(i):
-                rows = tile_rows(i)
-                pre = matmul(nrm[rows, :], l1[blk])
-                sq, t, half = gelu_half(pre)
-                act[rows, :] = (pre * half).astype(BF16)
-                slope = half + ((half * (1.0 - t)) * pre) * (GELU_C + (3.0 * GELU_C * GELU_K) * sq)
-                d_pre = (matmul_t(err_lo[rows, :], l2[blk]) * slope).astype(BF16)
-                dpre[rows, :] = d_pre
-                acc[rows, :] += matmul_t(d_pre, l1[blk])
+            behind = None
+            for rows in pieces + [None]:
+                if rows is not None:
+                    pre = matmul(nrm[rows, :], l1[blk])
+                    d_act = matmul_t(err_lo[rows, :], l2[blk])
+                if behind is not None:
+                    acc[behind[0], :] += matmul_t(behind[1], l1[blk])
+                if rows is not None:
+                    sq, t, half = gelu_half(pre)
+                    act[rows, :] = (pre * half).astype(BF16)
+                    slope = half + ((half * (1.0 - t)) * pre) * (GELU_C + (3.0 * GELU_C * GELU_K) * sq)
+                    d_pre = (d_act * slope).astype(BF16)
+                    dpre[rows, :] = d_pre
+                    behind = (rows, d_pre)
 
             @pl.when(k > 0)
             def _():

time: 670 us -> 666 us (level)
  no operation moved by 1% of the time
where the time goes in v7:
time: 666 us; the launch traced here: 665 us
  Pallas kernels  657 us (99%)
  local copies, waits for them, and re-layouts  7.49 us (1%)
    pallas_call x1, Pallas kernels, device_fn(): pl.pallas_call(functools.partial(kernel, dims), out_shape=(pltpu.VMEM((n_...  657 us

profile of v7, /device:TPU:0, one launch (start us, length us, event | category | flops | bytes accessed | tf_op | source)
XLA Modules:
  0.0 664.9 jit_solution(1496601484635469956)
XLA Ops:
  0.6 656.8 %gossip_sgd.1 = (f32[4,384,1536]{2,1,0:T(8,128)S(1)}, f32[12,512,384]{2,1,0:T(8,128)S(1)}, bf16[3,3,12,384,512]{4,3,2,1,0:T(8,128)(2,1)}, bf16[3,3,12,512,384]{4,3,2,1,0:T(8,128)(2,1)}) custom-call(f32[4,384,1536]{2,1,0:T(8,128)} %bitcast.8, f32[4,1536,384]{2,1,0:T(8,128)} %bitcast.9, bf16[3,2048,384]{2,1,0:T(8,128)(2,1)} %bitcast.10, ...), custom_call_target="tpu_custom_call" | custom-call | tf_op jit(solution)/shard_map/gossip_sgd/pallas_call | solution.py:400
  657.4 3.7 copy.8
  661.1 3.7 copy.9

commit v8 on v7

--- a/solution.py
+++ b/solution.py
@@ -40,7 +40,7 @@
 
 
 def kernel(dims, w1_hbm, w2_hbm, x_hbm, tgt_hbm, m1, m2, r1_hbm, r2_hbm,
-           l1, l2, hs, err, acc, tgt, ff, nrm, err_lo, nrm_t, err_t, head_two, tail_one, tail_two, st1, st2,
+           l1, l2, hs, err, acc, tgt, ff, nrm, err_lo, nrm_t, err_t, head_two, tail_one, tail_two, last_two, st1, st2,
            load_sem, data_sem, stage_sem, send_sem, recv_sem):
     n_rows, n_cols, n_steps, n_layers, batch, d_model, d_ff = dims
     f_blk = d_ff // CHUNKS
@@ -67,17 +67,17 @@
 
     wires = ((None, l1, r1_hbm, st1), (None, l2, r2_hbm, st2))
 
-    def sends(step, blk, mat, src=None):
+    def sends(step, blk, mat, src=None, dst=None):
         out = []
         for slot, peer in enumerate(peers):
             out.append(pltpu.make_async_remote_copy(
-                src_ref=wires[mat][1].at[blk] if src is None else src, dst_ref=wires[mat][2].at[step, slot, blk],
+                src_ref=wires[mat][1].at[blk] if src is None else src, dst_ref=wires[mat][2].at[step, slot, blk] if dst is None else dst.at[slot],
                 send_sem=send_sem.at[blk, mat, slot], recv_sem=recv_sem.at[step, blk, mat, slot],
                 device_id=peer, device_id_type=MESH))
         return out
 
-    def start_sends(step, blk, mat, src=None):
-        for cp in sends(step, blk, mat, src):
+    def start_sends(step, blk, mat, src=None, dst=None):
+        for cp in sends(step, blk, mat, src, dst):
             cp.start()
 
     def sent_early(blk):
@@ -355,8 +355,16 @@
         def _(blk):
             @pl.when(is_tail(blk))
             def _():
-                for mat in range(2):
-                    start_sends(step, blk, mat, tail_src(blk, mat))
+                final = jnp.logical_and(step == n_steps - 1, blk == n_blk - 1)
+                start_sends(step, blk, 0, tail_src(blk, 0))
+
+                @pl.when(jnp.logical_not(final))
+                def _():
+                    start_sends(step, blk, 1, tail_src(blk, 1))
+
+                @pl.when(final)
+                def _():
+                    start_sends(step, blk, 1, tail_src(blk, 1), last_two)
 
             @pl.when(jnp.logical_not(jnp.logical_or(sent_early(blk), is_tail(blk))))
             def _():
@@ -375,8 +383,16 @@
 
             @pl.when(turn)
             def _():
-                for mat in range(2):
-                    mix(n_steps - 1, blk, (mat,))
+                mix(n_steps - 1, blk, (0,))
+
+                @pl.when(blk < n_blk - 1)
+                def _():
+                    mix(n_steps - 1, blk, (1,))
+
+    for cp in sends(n_steps - 1, n_blk - 1, 1, None, last_two):
+        cp.wait_recv()
+    other = last_two[2].astype(F32)
+    m2[n_blk - 1] = (m2[n_blk - 1] + last_two[0].astype(F32) + last_two[1].astype(F32) + other + other) * 0.2
 
     @pl.loop(0, n_blk)
     def _(blk):
@@ -422,6 +438,7 @@
                 pltpu.VMEM((f_blk, d_model), BF16),
                 pltpu.VMEM((n_layers - 1, d_model, f_blk), BF16),
                 pltpu.VMEM((n_layers - 1, f_blk, d_model), BF16),
+                pltpu.VMEM((3, f_blk, d_model), BF16),
                 pltpu.VMEM((3, d_model, f_blk), BF16),
                 pltpu.VMEM((3, f_blk, d_model), BF16),
                 pltpu.SemaphoreType.DMA((n_blk, 2)),

time: 666 us -> 665 us (level)
  no operation moved by 1% of the time
where the time goes in v8:
time: 665 us; the launch traced here: 664 us
  Pallas kernels  655 us (98%)
  local copies, waits for them, and re-layouts  7.49 us (1%)
    pallas_call x1, Pallas kernels, device_fn(): pl.pallas_call(functools.partial(kernel, dims), out_shape=(pltpu.VMEM((n_...  655 us

profile of v8, /device:TPU:0, one launch (start us, length us, event | category | flops | bytes accessed | tf_op | source)
XLA Modules:
  0.0 663.6 jit_solution(12032996354316334780)
XLA Ops:
  0.6 655.5 %gossip_sgd.1 = (f32[4,384,1536]{2,1,0:T(8,128)S(1)}, f32[12,512,384]{2,1,0:T(8,128)S(1)}, bf16[3,3,12,384,512]{4,3,2,1,0:T(8,128)(2,1)}, bf16[3,3,12,512,384]{4,3,2,1,0:T(8,128)(2,1)}) custom-call(f32[4,384,1536]{2,1,0:T(8,128)} %bitcast.8, f32[4,1536,384]{2,1,0:T(8,128)} %bitcast.9, bf16[3,2048,384]{2,1,0:T(8,128)(2,1)} %bitcast.10, ...), custom_call_target="tpu_custom_call" | custom-call | tf_op jit(solution)/shard_map/gossip_sgd/pallas_call | solution.py:416
  656.1 3.7 copy.8
  659.9 3.7 copy.9
